TPU v7x, 32 devices: a whole 2x2x4 slice. The times are simulated.
32 devices in a mesh: seq: 16 (over z, y, x), ch: 2 (over core).
Axes of the slice: x: 2, y: 2, z: 4, core: 2. Of those that a mesh axis runs over, the one named last changes fastest.
Arguments:
- tokens: bfloat16 [2048, 8192], P('seq', 'ch'), may hold values from -6 to 6
- query_in: bfloat16 [2048, 8192], P('seq', 'ch'), may hold values from -6 to 6
- key_in: bfloat16 [2048, 8192], P('seq', 'ch'), may hold values from -6 to 6
- proj_in: bfloat16 [8192, 1536], P('ch', 'seq'), may hold values from -0.0625 to 0.0625
- proj_out: bfloat16 [1536, 8192], P('seq', 'ch'), may hold values from -0.15625 to 0.15625
- short_taps: float32 [3, 7, 8192], P(None, None, 'ch'), may hold values from -2.4 to 2.4
- residues: float32 [16, 8192], P(None, 'ch'), may hold values from -1.8 to 1.8
- mode_rates: float32 [16, 8192], P(None, 'ch'), may hold values from 0.00024414062 to 0.03
- skip_gain: float32 [8192], P('ch'), may hold values from -3 to 3
Outputs:
- operator_out: bfloat16 [2048, 8192], P('seq', 'ch')
All inputs are finite; a program needn't handle non-finite values.
Results may differ from a plain program's by a relative error of at most 0.0069.
Values may be sent and summed in bfloat16 or wider, within the bound.
A program may use at most 192 MiB of HBM per device.

v0:
```python
import jax
import jax.numpy as jnp
from jax import lax
from jax.sharding import PartitionSpec as P

precise = lax.Precision.HIGHEST


def carried_in(value, axis, join, neutral):
    count, mine = (lax.axis_size(axis), lax.axis_index(axis))
    pieces = jax.tree.map(lambda part: lax.all_gather(part, axis), value)
    total = jax.tree.map(
        lambda part, zero: jnp.full_like(part, 0) + jnp.asarray(zero, part.dtype), value, neutral
    )

    def turn(position, total):
        longer = join(total, jax.tree.map(lambda part: part[position], pieces))
        return jax.tree.map(lambda new, old: jnp.where(position < mine, new, old), longer, total)

    return lax.fori_loop(0, count - 1, turn, total)


def passed_along(value, axis, steps):
    count = lax.axis_size(axis)
    leading, last = (max(0, -steps), min(count, count - steps))
    return lax.ppermute(value, axis, [(source, source + steps) for source in range(leading, last)])


def short_filter(previous, current, filter_taps):
    margin_rows = filter_taps.shape[0] - 1
    length = current.shape[0]
    extended = jnp.concatenate([previous, current], axis=0).astype(jnp.float32)
    result = filter_taps[0] * extended[margin_rows : margin_rows + length]
    for offset in range(1, margin_rows + 1):
        result = (
            result
            + filter_taps[offset] * extended[margin_rows - offset : margin_rows - offset + length]
        )
    return result


def carry_states(earlier, later):
    return (earlier[0] * later[1] + later[0], earlier[1] * later[1])


def modal_convolve(mixed, residues, mode_rates):
    tok_rows = mixed.shape[0]
    signal = mixed.astype(jnp.float32)
    steps = jnp.arange(tok_rows, dtype=jnp.int32)
    lower = (steps[:, None] >= steps[None, :]).astype(jnp.float32)
    centred = (steps.astype(jnp.float32) - 0.5 * tok_rows)[:, None]
    local_total = jnp.zeros(signal.shape, jnp.float32)
    end_list = []
    for mode_index in range(residues.shape[0]):
        rate_mode = mode_rates[mode_index]
        weight = residues[mode_index] * jnp.sqrt(rate_mode)
        rising = jnp.exp(rate_mode * centred)
        falling = jnp.exp(-rate_mode * centred)
        running = falling * jnp.dot(lower, rising * signal, precision=precise)
        local_total = local_total + weight * running
        end_list.append(running[tok_rows - 1])
    end_states = jnp.stack(end_list)
    block_decay = jnp.exp(-mode_rates * tok_rows)
    identity = (jnp.zeros(end_states.shape, jnp.float32), jnp.ones(end_states.shape, jnp.float32))
    carried, _ = carried_in((end_states, block_decay), "seq", carry_states, identity)
    after = (steps.astype(jnp.float32) + 1.0)[:, None]
    for mode_index in range(residues.shape[0]):
        rate_mode = mode_rates[mode_index]
        weight = residues[mode_index] * jnp.sqrt(rate_mode)
        local_total = local_total + weight * carried[mode_index] * jnp.exp(-rate_mode * after)
    rounded = lax.optimization_barrier(local_total.astype(jnp.bfloat16))
    return rounded.astype(jnp.float32)


def per_device(
    tokens, query_in, key_in, proj_in, proj_out, short_taps, residues, mode_rates, skip_gain
):
    tok_rows = tokens.shape[0]
    margin_rows = short_taps.shape[1] - 1
    partial_value = jnp.dot(
        tokens,
        lax.all_gather(proj_in, "seq", axis=1, tiled=True),
        preferred_element_type=jnp.float32,
    )
    low_rank = lax.psum(partial_value, "ch").astype(jnp.bfloat16)
    value_full = jnp.dot(
        low_rank,
        lax.all_gather(proj_out, "seq", axis=0, tiled=True),
        preferred_element_type=jnp.float32,
    )
    value_proj = value_full.astype(jnp.bfloat16)
    edges = jnp.stack(
        [
            query_in[tok_rows - margin_rows :],
            key_in[tok_rows - margin_rows :],
            value_proj[tok_rows - margin_rows :],
        ]
    )
    arrived_edges = passed_along(edges, "seq", 1)
    query_previous = arrived_edges[0]
    key_previous = arrived_edges[1]
    value_previous = arrived_edges[2]
    query_short = short_filter(query_previous, query_in, short_taps[0])
    key_short = short_filter(key_previous, key_in, short_taps[1])
    value_short = short_filter(value_previous, value_proj, short_taps[2])
    mixed = (key_short * value_short).astype(jnp.bfloat16)
    convolved_tokens = modal_convolve(mixed, residues, mode_rates)
    return (query_short * (convolved_tokens + skip_gain * mixed.astype(jnp.float32))).astype(
        jnp.bfloat16
    )


def solution(mesh):
    placed = (
        P("seq", "ch"),
        P("seq", "ch"),
        P("seq", "ch"),
        P("ch", "seq"),
        P("seq", "ch"),
        P(None, None, "ch"),
        P(None, "ch"),
        P(None, "ch"),
        P("ch"),
    )
    return jax.shard_map(
        per_device, mesh=mesh, in_specs=placed, out_specs=P("seq", "ch"), check_vma=False
    )
```

profile of v0, /device:TPU:0, one launch (start us, length us, event | category | flops | bytes accessed | tf_op | source)
XLA Modules:
  0.0 516.6 jit_solution(9154989654127327355)
XLA Ops:
  14.1 150.2 %all-gather.7.cloned.1.call-done = bf16[4096,1536]{0,1:T(8,128)(2,1)} async-done(((bf16[4096,96]{0,1:T(8,128)(2,1)}), bf16[4096,1536]{0,1:T(8,128)(2,1)}) %all-gather.7.cloned.1.call-update) | async-done | bytes 12582928 | tf_op jit(solution)/shard_map/all_gather | solution.py:82
  164.3 8.8 %fusion.92 = f32[128,1536]{1,0:T(8,128)S(1)} fusion(bf16[128,4096]{1,0:T(8,128)(2,1)S(1)} %copy-done, bf16[4096,1536]{0,1:T(8,128)(2,1)} %all-gather.7.cloned.1.call-done), kind=kOutput, calls=%fused_computation.212 | convolution fusion | flops 1610612736 | bytes 14417920 | tf_op jit(solution)/shard_map/dot_general | solution.py:80
  173.1 5.5 %all-reduce.1 = bf16[128,1536]{1,0:T(8,128)(2,1)S(1)} all-reduce(f32[128,1536]{1,0:T(8,128)S(1)} %fusion.92), channel_id=1, replica_groups=mesh['seq'=16,'ch'=2] {'ch'}, use_global_device_ids=true, to_apply=%region_0.0 | all-reduce | flops 196608 | bytes 1179648 | tf_op jit(solution)/shard_map/psum | solution.py:85
  178.7 138.0 %all-gather.9.cloned.1.call-done = bf16[1536,4096]{1,0:T(8,128)(2,1)} async-done(((bf16[96,4096]{1,0:T(8,128)(2,1)}), bf16[1536,4096]{1,0:T(8,128)(2,1)}) %all-gather.9.cloned.1.call-update) | async-done | bytes 12582928 | tf_op jit(solution)/shard_map/all_gather | solution.py:88
  316.7 6.4 %convolution_convert_fusion = bf16[128,4096]{1,0:T(8,128)(2,1)S(1)} fusion(bf16[1536,4096]{1,0:T(8,128)(2,1)} %all-gather.9.cloned.1.call-done, bf16[128,1536]{1,0:T(8,128)(2,1)S(1)} %all-reduce.1), kind=kOutput, calls=%fused_computation.36 | convolution fusion | flops 1611137024 | bytes 14024704 | tf_op jit(solution)/shard_map/dot_general | solution.py:86
  323.2 3.4 collective-permute-start
  327.6 4.3 collective-permute-done
  333.7 3.7 fusion.6
  337.5 2.0 convolution_multiply_fusion.3
  339.5 1.9 convolution_multiply_fusion.2
  341.5 1.9 convolution_multiply_fusion.1
  343.5 1.9 convolution_multiply_fusion.15
  345.6 1.9 convolution_multiply_fusion.14
  347.6 1.9 convolution_multiply_fusion.13
  349.6 2.1 convolution_multiply_fusion.12
  351.9 1.9 convolution_multiply_fusion.11
  358.0 1.9 convolution_multiply_fusion.8
  362.0 2.2 convolution_multiply_fusion.6
  364.3 1.9 convolution_multiply_fusion.5
  375.5 18.6 %all-gather.11.cloned.1.call-done = f32[256,4096]{1,0:T(8,128)} async-done(((f32[16,4096]{1,0:T(8,128)}), f32[256,4096]{1,0:T(8,128)}) %all-gather.11.cloned.1.call-update) | async-done | bytes 4194320 | tf_op jit(solution)/shard_map/all_gather | solution.py:11
  394.1 76.8 %all-gather.13.cloned.1.call-done = f32[256,4096]{1,0:T(8,128)} async-done(((f32[16,4096]{1,0:T(8,128)}), f32[256,4096]{1,0:T(8,128)}) %all-gather.13.cloned.1.call-update) | async-done | bytes 4194320 | tf_op jit(solution)/shard_map/all_gather | solution.py:11
  471.1 19.2 %while.14 = (s32[]{:T(128)}, f32[16,4096]{1,0:T(8,128)S(1)}, s32[]{:T(128)}, f32[16,16,4096]{2,1,0:T(8,128)}, f32[16,16,4096]{2,1,0:T(8,128)}, /*index=5*/s32[]{:T(128)}, s32[]{:T(128)}) while((s32[]{:T(128)}, f32[16,4096]{1,0:T(8,128)S(1)}, s32[]{:T(128)}, f32[16,16,4096]{2,1,0:T(8,128)}, f32[16,16,4096]{2,1,0:T(8,128)}, ...), condition=%wide.region_2.3_spmd.clone, body=%wide.region_1.2_spmd.clone.sunk | while | flops 262148 | bytes 1048677 | solution.py:20
  491.5 15.0 %add_convert_fusion = bf16[128,4096]{1,0:T(8,128)(2,1)S(1)} fusion(f32[128,4096]{1,0:T(8,128)} %copy-done.20, f32[128,4096]{1,0:T(8,128)} %copy-done.7, f32[128,4096]{1,0:T(8,128)} %copy-done.6, f32[128,4096]{1,0:T(8,128)} %copy-done.5, f32[128,4096]{1,0:T(8,128)} %copy-done.19, f32[128,4096]{1,0:T(8,128)} %copy-done.18, f32[128,4096]{1,0:T(8,128)} %copy-done.17, ...), kind=kLoop, calls=%fused_computation.81 | loop fusion | flops 41943040 | bytes 35389952 | tf_op jit(solution)/shard_map/convert_element_type | solution.py:71
  506.7 2.9 fusion.3
  (247 shorter events, 45.6 us)
Async XLA Ops:
  6.5 157.8 %copy-start = (bf16[128,4096]{1,0:T(8,128)(2,1)S(1)}, bf16[128,4096]{1,0:T(8,128)(2,1)}, u32[]{:S(2)}) copy-start(bf16[128,4096]{1,0:T(8,128)(2,1)} %param.11) | copy-start | bytes 3145732
  6.5 157.7 %all-gather.7.cloned.1.call-start = ((), (), s32[]{:S(2)}) async-start(), calls=%async_computation | async-start | bytes 13369344 | tf_op jit(solution)/shard_map/all_gather | solution.py:82
  7.3 309.4 %all-gather.9.cloned.1.call-start = ((), (), s32[]{:S(2)}) async-start(), calls=%async_computation.1 | async-start | bytes 13369344 | tf_op jit(solution)/shard_map/all_gather | solution.py:88
  8.0 386.1 %all-gather.11.cloned.1.call-start = ((), (), s32[]{:S(2)}) async-start(), calls=%async_computation.2 | async-start | bytes 4456448 | tf_op jit(solution)/shard_map/all_gather | solution.py:11
  9.8 461.2 %all-gather.13.cloned.1.call-start = ((), (), s32[]{:S(2)}) async-start(), calls=%async_computation.3 | async-start | bytes 4456448 | tf_op jit(solution)/shard_map/all_gather | solution.py:11
  178.6 144.5 %copy-start.24 = (bf16[1,6,4096]{2,1,0:T(8,128)(2,1)S(1)}, bf16[1,6,4096]{2,1,0:T(8,128)(2,1)}, u32[]{:S(2)}) copy-start(bf16[1,6,4096]{2,1,0:T(8,128)(2,1)} %get-tuple-element.242) | copy-start | bytes 147460
  178.7 144.5 %copy-start.25 = (bf16[1,6,4096]{2,1,0:T(8,128)(2,1)S(1)}, bf16[1,6,4096]{2,1,0:T(8,128)(2,1)}, u32[]{:S(2)}) copy-start(bf16[1,6,4096]{2,1,0:T(8,128)(2,1)} %get-tuple-element.243) | copy-start | bytes 147460
  323.2 8.7 %collective-permute-start = (bf16[3,6,4096]{2,1,0:T(8,128)(2,1)S(1)}, bf16[3,6,4096]{2,1,0:T(8,128)(2,1)S(1)}, u32[]{:S(2)}, u32[]{:S(2)}) collective-permute-start(bf16[3,6,4096]{2,1,0:T(8,128)(2,1)S(1)} %pad_maximum_fusion), channel_id=1, source_target_pairs={{0,2},{2,4},{4,6},{6,8},{8,10},{10,12},{12,14},{14,16},{16,18},{18... | collective-permute-start | bytes 442376 | tf_op jit(solution)/shard_map/ppermute | solution.py:26
  337.4 30.9 %copy-start.2 = (bf16[128,4096]{1,0:T(8,128)(2,1)}, bf16[128,4096]{1,0:T(8,128)(2,1)S(1)}, u32[]{:S(2)}) copy-start(bf16[128,4096]{1,0:T(8,128)(2,1)S(1)} %fusion.6) | copy-start | bytes 3145732
  471.0 20.3 %copy-start.27 = (f32[1,4096]{1,0:T(1,128)S(1)}, f32[1,4096]{1,0:T(1,128)}, u32[]{:S(2)}) copy-start(f32[1,4096]{1,0:T(1,128)} %get-tuple-element.208) | copy-start | bytes 49156
  471.0 20.4 %copy-start.29 = (f32[1,4096]{1,0:T(1,128)S(1)}, f32[1,4096]{1,0:T(1,128)}, u32[]{:S(2)}) copy-start(f32[1,4096]{1,0:T(1,128)} %get-tuple-element.209) | copy-start | bytes 49156
  471.0 20.4 %copy-start.31 = (f32[1,4096]{1,0:T(1,128)S(1)}, f32[1,4096]{1,0:T(1,128)}, u32[]{:S(2)}) copy-start(f32[1,4096]{1,0:T(1,128)} %get-tuple-element.210) | copy-start | bytes 49156
  471.0 20.4 %copy-start.33 = (f32[1,4096]{1,0:T(1,128)S(1)}, f32[1,4096]{1,0:T(1,128)}, u32[]{:S(2)}) copy-start(f32[1,4096]{1,0:T(1,128)} %get-tuple-element.211) | copy-start | bytes 49156
  471.0 20.4 %copy-start.35 = (f32[1,4096]{1,0:T(1,128)S(1)}, f32[1,4096]{1,0:T(1,128)}, u32[]{:S(2)}) copy-start(f32[1,4096]{1,0:T(1,128)} %get-tuple-element.212) | copy-start | bytes 49156
  471.0 20.4 %copy-start.37 = (f32[1,4096]{1,0:T(1,128)S(1)}, f32[1,4096]{1,0:T(1,128)}, u32[]{:S(2)}) copy-start(f32[1,4096]{1,0:T(1,128)} %get-tuple-element.213) | copy-start | bytes 49156
  471.0 20.4 %copy-start.39 = (f32[1,4096]{1,0:T(1,128)S(1)}, f32[1,4096]{1,0:T(1,128)}, u32[]{:S(2)}) copy-start(f32[1,4096]{1,0:T(1,128)} %get-tuple-element.214) | copy-start | bytes 49156
  471.0 20.4 %copy-start.41 = (f32[1,4096]{1,0:T(1,128)S(1)}, f32[1,4096]{1,0:T(1,128)}, u32[]{:S(2)}) copy-start(f32[1,4096]{1,0:T(1,128)} %get-tuple-element.215) | copy-start | bytes 49156
  471.0 20.4 %copy-start.43 = (f32[1,4096]{1,0:T(1,128)S(1)}, f32[1,4096]{1,0:T(1,128)}, u32[]{:S(2)}) copy-start(f32[1,4096]{1,0:T(1,128)} %get-tuple-element.216) | copy-start | bytes 49156
  471.0 20.4 %copy-start.45 = (f32[1,4096]{1,0:T(1,128)S(1)}, f32[1,4096]{1,0:T(1,128)}, u32[]{:S(2)}) copy-start(f32[1,4096]{1,0:T(1,128)} %get-tuple-element.217) | copy-start | bytes 49156
  471.0 20.4 %copy-start.47 = (f32[1,4096]{1,0:T(1,128)S(1)}, f32[1,4096]{1,0:T(1,128)}, u32[]{:S(2)}) copy-start(f32[1,4096]{1,0:T(1,128)} %get-tuple-element.218) | copy-start | bytes 49156
  471.0 20.4 %copy-start.49 = (f32[1,4096]{1,0:T(1,128)S(1)}, f32[1,4096]{1,0:T(1,128)}, u32[]{:S(2)}) copy-start(f32[1,4096]{1,0:T(1,128)} %get-tuple-element.219) | copy-start | bytes 49156
  471.0 20.4 %copy-start.51 = (f32[1,4096]{1,0:T(1,128)S(1)}, f32[1,4096]{1,0:T(1,128)}, u32[]{:S(2)}) copy-start(f32[1,4096]{1,0:T(1,128)} %get-tuple-element.220) | copy-start | bytes 49156
  471.1 20.4 %copy-start.53 = (f32[1,4096]{1,0:T(1,128)S(1)}, f32[1,4096]{1,0:T(1,128)}, u32[]{:S(2)}) copy-start(f32[1,4096]{1,0:T(1,128)} %get-tuple-element.221) | copy-start | bytes 49156
  471.1 20.4 %copy-start.55 = (f32[1,4096]{1,0:T(1,128)S(1)}, f32[1,4096]{1,0:T(1,128)}, u32[]{:S(2)}) copy-start(f32[1,4096]{1,0:T(1,128)} %get-tuple-element.222) | copy-start | bytes 49156
  (73 other events, 311.3 us)
Sparse Core Ops, SparseCore 0:
  10.1 154.1 all-gather.6
  167.1 149.5 all-gather.8
  319.5 74.5 all-gather.10
  396.7 74.1 all-gather.12
where the time goes:
time: 524 us; the launch traced here: 517 us
  waiting for transfers between devices  389 us (74%)
  other arithmetic  46.9 us (9%)
  matrix products  46.7 us (9%)
  between operations  15.2 us (3%)
  local copies, waits for them, and re-layouts  9.07 us (2%)
  blocking collectives  5.51 us (1%)
    all_gather x1, waiting for transfers between devices, per_device(): lax.all_gather(proj_in, 'seq', axis=1, tiled=True)  150 us
    all_gather x1, waiting for transfers between devices, per_device(): lax.all_gather(proj_out, 'seq', axis=0, tiled=True)  138 us
    all_gather x2, waiting for transfers between devices, carried_in(): pieces = jax.tree.map(lambda part: lax.all_gather(part, axis), value)  95.4 us
    dot_general x16, matrix products, modal_convolve(): running = falling * jnp.dot(lower, rising * signal, precision=precise)  31.5 us
    select_n x15, other arithmetic, turn(): jnp.where(position < mine, new, old)  18.8 us
    convert_element_type x1, other arithmetic, modal_convolve(): rounded = lax.optimization_barrier(local_total.astype(jnp.bfloat16))  15 us
  transfers between devices with their start and end apart: 5, of which 5 were waited for; matrix products, arithmetic and copies ran while one was open for 12% of the time, Pallas kernels for 0%

commit v1 on v0

--- a/solution.py
+++ b/solution.py
@@ -1,7 +1,350 @@
+import functools
+
 import jax
 import jax.numpy as jnp
 from jax import lax
+from jax.experimental import pallas as pl
+from jax.experimental.pallas import tpu as pltpu
 from jax.sharding import PartitionSpec as P
+
+MESH = pl.DeviceIdType.MESH
+VMEM = pl.BlockSpec(memory_space=pltpu.VMEM)
+ANY = pl.BlockSpec(memory_space=pl.ANY)
+GROUP = 4
+
+
+def flip(position):
+    return position + (position // 2) * (1 - 2 * (position % 2))
+
+
+def where_am_i():
+    me = lax.axis_index("seq")
+    return me // GROUP, me % GROUP
+
+
+def device(plane, spot):
+    return {"seq": plane * GROUP + spot}
+
+
+def remote(source, target, sems, index, place):
+    return pltpu.make_async_remote_copy(
+        src_ref=source, dst_ref=target, send_sem=sems[0].at[index], recv_sem=sems[1].at[index],
+        device_id=place, device_id_type=MESH,
+    )
+
+
+def greet(places):
+    barrier = pltpu.get_barrier_semaphore()
+    for place in places:
+        pl.semaphore_signal(barrier, inc=1, device_id=place, device_id_type=MESH)
+    pl.semaphore_wait(barrier, len(places))
+
+
+class Ring:
+    def __init__(self, own, slot, sems, base, mine, left, right, left_dev, right_dev):
+        self.first = [
+            remote(own(0), slot(mine, 0), sems, base, right_dev),
+            remote(own(1), slot(mine, 1), sems, base + 1, left_dev),
+            remote(own(1), slot(mine, 1), sems, base + 2, right_dev),
+            remote(own(0), slot(mine, 0), sems, base + 3, left_dev),
+        ]
+        self.onward = [
+            remote(slot(left, 0), slot(left, 0), sems, base + 4, right_dev),
+            remote(slot(right, 1), slot(right, 1), sems, base + 5, left_dev),
+        ]
+
+    def start(self):
+        for copy in self.first:
+            copy.start()
+
+    def relay(self):
+        for arrived, onward in zip(self.first[:2], self.onward):
+            arrived.wait_recv()
+            onward.start()
+
+    def finish(self):
+        for copy in self.first[2:] + self.onward:
+            copy.wait_recv()
+        for copy in self.first + self.onward:
+            copy.wait_send()
+
+
+def rings():
+    plane, spot = where_am_i()
+    turn = flip(spot)
+    left, right = flip((turn + GROUP - 1) % GROUP), flip((turn + 1) % GROUP)
+    flat = (spot, left, right, device(plane, left), device(plane, right))
+    below, above = (plane + GROUP - 1) % GROUP, (plane + 1) % GROUP
+    tall = (plane, below, above, device(below, spot), device(above, spot))
+    return plane, spot, flat, tall
+
+
+def everyone(plane, spot, tall):
+    return [device(plane, (spot + step) % GROUP) for step in range(1, GROUP)] + [tall[3], tall[4]]
+
+
+def swap(piece, slot, sems, base, plane, spot):
+    copies = []
+    for step in range(1, GROUP):
+        peer = (spot + step) % GROUP
+        copies.append(remote(piece(peer), slot(spot), sems, base + step - 1, device(plane, peer)))
+    return copies
+
+
+def gather_first(tok, pin, pout, tok_all, pin_all, rows_late, rows_early, pieces, send, recv, local):
+    plane, spot, flat, tall = rings()
+    sems = (send, recv)
+    width = pieces.shape[-1]
+    greet(everyone(plane, spot, tall))
+
+    def piece(peer):
+        return pout.at[:, pl.ds(pl.multiple_of(peer * width, width), width)]
+
+    half_tok, half_pin = tok.shape[0] // 2, pin.shape[0] // 2
+    moved = swap(piece, lambda s: pieces.at[s], sems, 18, plane, spot)
+    for copy in moved:
+        copy.start()
+    tokens_ring = Ring(
+        lambda h: tok.at[pl.ds(h * half_tok, half_tok)],
+        lambda s, h: tok_all.at[s, pl.ds(h * half_tok, half_tok)], sems, 0, *flat)
+    pin_ring = Ring(
+        lambda h: pin.at[pl.ds(h * half_pin, half_pin)],
+        lambda s, h: pin_all.at[s, pl.ds(h * half_pin, half_pin)], sems, 6, *tall)
+    tokens_ring.start()
+    pin_ring.start()
+    keep = [
+        pltpu.make_async_copy(tok, tok_all.at[spot], local.at[0]),
+        pltpu.make_async_copy(pin, pin_all.at[plane], local.at[1]),
+        pltpu.make_async_copy(piece(spot), pieces.at[spot], local.at[2]),
+    ]
+    for copy in keep:
+        copy.start()
+    pin_ring.relay()
+    keep[2].wait()
+    for copy in moved:
+        copy.wait_recv()
+    rows_ring = Ring(
+        lambda h: pieces.at[h], lambda s, h: rows_early.at[h, s], sems, 12, *tall)
+    rows_ring.start()
+    last = [
+        pltpu.make_async_copy(pieces.at[pl.ds(2, 2)], rows_late, local.at[3]),
+        pltpu.make_async_copy(pieces.at[0], rows_early.at[0, plane], local.at[4]),
+        pltpu.make_async_copy(pieces.at[1], rows_early.at[1, plane], local.at[5]),
+    ]
+    for copy in last:
+        copy.start()
+    tokens_ring.relay()
+    rows_ring.relay()
+    pin_ring.finish()
+    tokens_ring.finish()
+    rows_ring.finish()
+    for copy in moved:
+        copy.wait_send()
+    for copy in keep[:2] + last:
+        copy.wait()
+
+
+def gather_second(low, rows, key, low_all, rows_all, key_all, send, recv, local):
+    plane, spot, flat, tall = rings()
+    sems = (send, recv)
+    width, ranks, half = key_all.shape[-1], low.shape[1], low.shape[0] // 2
+    greet(everyone(plane, spot, tall))
+
+    def columns(s):
+        return pl.ds(pl.multiple_of(s * ranks, ranks), ranks)
+
+    def piece(peer):
+        return key.at[:, pl.ds(pl.multiple_of(peer * width, width), width)]
+
+    low_ring = Ring(
+        lambda h: low.at[pl.ds(h * half, half)],
+        lambda s, h: low_all.at[pl.ds(h * half, half), columns(s)], sems, 0, *flat)
+    rows_ring = Ring(lambda h: rows.at[h], lambda s, h: rows_all.at[h, s], sems, 6, *tall)
+    moved = swap(piece, lambda s: key_all.at[s], sems, 12, plane, spot)
+    low_ring.start()
+    rows_ring.start()
+    keep = [
+        pltpu.make_async_copy(low, low_all.at[:, columns(spot)], local.at[0]),
+        pltpu.make_async_copy(rows.at[0], rows_all.at[0, plane], local.at[1]),
+        pltpu.make_async_copy(rows.at[1], rows_all.at[1, plane], local.at[2]),
+        pltpu.make_async_copy(piece(spot), key_all.at[spot], local.at[3]),
+    ]
+    for copy in keep:
+        copy.start()
+    low_ring.relay()
+    for copy in moved:
+        copy.start()
+    rows_ring.relay()
+    low_ring.finish()
+    rows_ring.finish()
+    for copy in moved:
+        copy.wait_recv()
+    for copy in moved:
+        copy.wait_send()
+    for copy in keep:
+        copy.wait()
+
+
+def give_back(mine, out, send, recv, local):
+    plane, spot = where_am_i()
+    rows, width = out.shape[0], mine.shape[1]
+    greet([device(plane, (spot + step) % GROUP) for step in range(1, GROUP)])
+
+    def piece(peer):
+        return mine.at[pl.ds(pl.multiple_of(peer * rows, rows), rows)]
+
+    def slot(s):
+        return out.at[:, pl.ds(pl.multiple_of(s * width, width), width)]
+
+    moved = swap(piece, slot, (send, recv), 0, plane, spot)
+    for copy in moved:
+        copy.start()
+    keep = pltpu.make_async_copy(piece(spot), slot(spot), local.at[0])
+    keep.start()
+    for copy in moved:
+        copy.wait_recv()
+    for copy in moved:
+        copy.wait_send()
+    keep.wait()
+
+
+def talk(kernel, shapes, in_specs, scratch, copies, locals_, ident):
+    one = not isinstance(shapes, (list, tuple))
+    return pl.pallas_call(
+        kernel,
+        out_shape=shapes,
+        in_specs=in_specs,
+        out_specs=ANY if one else [ANY] * len(shapes),
+        scratch_shapes=scratch + [
+            pltpu.SemaphoreType.DMA((copies,)),
+            pltpu.SemaphoreType.DMA((copies,)),
+            pltpu.SemaphoreType.DMA((locals_,)),
+        ],
+        compiler_params=pltpu.CompilerParams(collective_id=ident, has_side_effects=True),
+    )
+
+
+def end_states(mixed, decay, spread, states):
+    rows, (modes, tall, lanes) = mixed.shape[0], decay.shape
+
+    @pl.loop(0, rows // 16)
+    def _(block):
+        start = pl.multiple_of(block * 16, 16)
+        for column in range(tall):
+            tile = mixed[pl.ds(start, 16), column * lanes:(column + 1) * lanes]
+            spread[pl.ds(start * tall + column, 16, stride=tall), :] = tile.astype(jnp.float32)
+
+    rates = [decay[mode] for mode in range(modes)]
+
+    def step(at, held):
+        for part in range(8):
+            value = spread[pl.ds(pl.multiple_of((at * 8 + part) * tall, tall), tall), :]
+            held = [h * r + value for h, r in zip(held, rates)]
+        return held
+
+    held = lax.fori_loop(0, rows // 8, step, [jnp.zeros((tall, lanes), jnp.float32)] * modes)
+    for mode in range(modes):
+        states[mode] = held[mode]
+
+
+def run_states(spread, carried, decay, weight, skip, out, kept):
+    modes, tall, lanes = decay.shape
+    rows = out.shape[0]
+    rates = [decay[mode] for mode in range(modes)]
+    weights = [weight[mode] for mode in range(modes)]
+    gain = skip[...]
+
+    def step(at, held):
+        for part in range(4):
+            place = pl.ds(pl.multiple_of((at * 4 + part) * tall, tall), tall)
+            value = spread[place, :]
+            held = [h * r + value for h, r in zip(held, rates)]
+            terms = [h * w for h, w in zip(held, weights)]
+            while len(terms) > 1:
+                terms = [a + b for a, b in zip(terms[::2], terms[1::2])]
+            rounded = terms[0].astype(jnp.bfloat16).astype(jnp.float32)
+            kept[place, :] = rounded + gain * value
+        return held
+
+    lax.fori_loop(0, rows // 4, step, [carried[mode] for mode in range(modes)])
+
+    @pl.loop(0, rows // 16)
+    def _(block):
+        start = pl.multiple_of(block * 16, 16)
+        for column in range(tall):
+            tile = kept[pl.ds(start * tall + column, 16, stride=tall), :]
+            out[pl.ds(start, 16), column * lanes:(column + 1) * lanes] = tile.astype(jnp.bfloat16)
+
+
+def planes_device(
+    tokens, query_in, key_in, proj_in, proj_out, short_taps, residues, mode_rates, skip_gain
+):
+    rows, channels = tokens.shape
+    ranks = proj_in.shape[1]
+    modes = residues.shape[0]
+    margin_rows = short_taps.shape[1] - 1
+    width, all_rows = channels // GROUP, rows * GROUP
+    tall = width // 128
+    half = jnp.bfloat16
+    shape = jax.ShapeDtypeStruct
+    plane, spot = where_am_i()
+    query_previous = passed_along(query_in[rows - margin_rows:], "seq", 1)
+
+    tok_all, pin_all, late, early = talk(
+        gather_first,
+        [shape((GROUP, rows, channels), half), shape((GROUP, ranks, channels), half),
+         shape((2, ranks, width), half), shape((2, GROUP, ranks, width), half)],
+        [VMEM] * 3, [pltpu.VMEM((GROUP, ranks, width), half)], 21, 6, 1,
+    )(tokens, proj_in.T, proj_out)
+    partial_value = lax.dot_general(
+        tok_all.reshape(all_rows, channels), pin_all.reshape(GROUP * ranks, channels),
+        (((1,), (1,)), ((), ())), preferred_element_type=jnp.float32)
+    low_rank = lax.psum(partial_value, "ch").astype(half)
+    low_all, rest, key_all = talk(
+        gather_second,
+        [shape((all_rows, GROUP * GROUP * ranks), half), shape((2, GROUP, ranks, width), half),
+         shape((GROUP, rows, width), half)],
+        [VMEM] * 3, [], 15, 4, 2,
+    )(low_rank, late, key_in)
+    factor = jnp.concatenate([early, rest], axis=0).reshape(GROUP * GROUP * ranks, width)
+    value = jnp.dot(low_all, factor, preferred_element_type=jnp.float32).astype(half)
+    key = key_all.reshape(all_rows, width)
+
+    def mine(part):
+        return lax.dynamic_slice_in_dim(part, spot * width, width, part.ndim - 1)
+
+    taps, rates, weights = mine(short_taps[1:]), mine(mode_rates), mine(residues)
+    edges = passed_along(
+        jnp.stack([key[all_rows - margin_rows:], value[all_rows - margin_rows:]]), "seq", GROUP)
+    mixed = (
+        short_filter(edges[0], key, taps[0]) * short_filter(edges[1], value, taps[1])
+    ).astype(half)
+    tiles = (modes, tall, 128)
+    weights = (weights * jnp.sqrt(rates)).reshape(tiles)
+    rates = rates.reshape(tiles)
+    decay = jnp.exp(-rates)
+    spread, states = pl.pallas_call(
+        end_states,
+        out_shape=[shape((all_rows * tall, 128), jnp.float32), shape(tiles, jnp.float32)],
+        in_specs=[VMEM] * 2, out_specs=[VMEM] * 2,
+    )(mixed, decay)
+    count = lax.axis_size("seq") // GROUP
+    groups = [[at * GROUP + s for at in range(count)] for s in range(GROUP)]
+    ends = lax.all_gather(states, "seq", axis_index_groups=groups)
+    carried = jnp.zeros(tiles, jnp.float32)
+    block = jnp.exp(-rates * all_rows)
+    for at in range(count - 1):
+        carried = jnp.where(at < plane, carried * block + ends[at], carried)
+    mixed_out = pl.pallas_call(
+        run_states,
+        out_shape=shape((all_rows, width), half),
+        in_specs=[VMEM] * 5, out_specs=VMEM,
+        scratch_shapes=[pltpu.VMEM((all_rows * tall, 128), jnp.float32)],
+    )(spread, carried, decay, weights, mine(skip_gain).reshape(tall, 128))
+    given = talk(give_back, shape((rows, channels), half), [VMEM], [], 3, 1, 3)(mixed_out)
+    query_short = short_filter(query_previous, query_in, short_taps[0])
+    return (query_short * given.astype(jnp.float32)).astype(half)
+
 
 precise = lax.Precision.HIGHEST
 
@@ -110,6 +453,18 @@
     )
 
 
+def chosen(mesh):
+    def run(*args):
+        rows, channels = args[0].shape
+        ranks = args[3].shape[1]
+        square = mesh.shape["seq"] == GROUP * GROUP
+        whole = channels % (GROUP * 1024) == 0 and ranks % 32 == 0 and rows % 32 == 0
+        fits = (GROUP * ranks) % 128 == 0 and channels == GROUP * 1024
+        return (planes_device if square and whole and fits else per_device)(*args)
+
+    return run
+
+
 def solution(mesh):
     placed = (
         P("seq", "ch"),
@@ -123,5 +478,5 @@
         P("ch"),
     )
     return jax.shard_map(
-        per_device, mesh=mesh, in_specs=placed, out_specs=P("seq", "ch"), check_vma=False
-    )
+        chosen(mesh), mesh=mesh, in_specs=placed, out_specs=P("seq", "ch"), check_vma=False
+    )

time: 524 us -> 200 us (0.38); the launches traced: 517 us -> 200 us
  waiting for transfers between devices: 389 us -> 0.01 us
  Pallas kernels: 0 us -> 142 us
  matrix products: 46.7 us -> 7.3 us
  other arithmetic: 46.9 us -> 13.5 us
  blocking collectives: 5.51 us -> 20.6 us
  between operations: 15.2 us -> 0.38 us
    all_gather x4 -> x0, waiting for transfers between devices: 384 us -> none  [the longest x1 150 us: per_device(): lax.all_gather(proj_in, 'seq', axis=1, tiled=True)]
    pallas_call x0 -> x5, Pallas kernels: none -> 142 us  [the longest x1 84 us: planes_device(): talk(gather_first, [shape((GROUP, rows, channels), half), shape((GROUP, r...]
    dot_general x18 -> x2, matrix products: 46.7 us -> 7.3 us  [the longest x1 5.51 us: planes_device(): lax.dot_general(tok_all.reshape(all_rows, channels), pin_all.reshape(GROU...]
    select_n x15 -> x1, other arithmetic: 18.8 us -> 0.65 us  [planes_device(): carried = jnp.where(at < plane, carried * block + ends[at], carried)]
    convert_element_type x3 -> x2, other arithmetic: 21.6 us -> 7.04 us  [the longest x1 4.33 us: planes_device(): mixed = (short_filter(edges[0], key, taps[0]) * short_filter(edges[1], va...]
    all_gather x0 -> x1, blocking collectives: none -> 14.5 us  [planes_device(): ends = lax.all_gather(states, 'seq', axis_index_groups=groups)]
  transfers between devices with their start and end apart: 5 -> 2, of which waited for: 5 -> 0; matrix products, arithmetic and copies ran while one was open for 12% -> 8% of each run, Pallas kernels for 0% -> 13%
where the time goes in v1:
time: 200 us
  Pallas kernels  142 us (71%)
  blocking collectives  20.6 us (10%)
  other arithmetic  13.5 us (7%)
  local copies, waits for them, and re-layouts  8.54 us (4%)
  starting transfers between devices  7.53 us (4%)
  matrix products  7.3 us (4%)
    pallas_call x1, Pallas kernels, planes_device(): talk(gather_first, [shape((GROUP, rows, channels), half), shape((GROUP, r...  84 us
    pallas_call x1, Pallas kernels, planes_device(): talk(gather_second, [shape((all_rows, GROUP * GROUP * ranks), half), shap...  31.9 us
    all_gather x1, blocking collectives, planes_device(): ends = lax.all_gather(states, 'seq', axis_index_groups=groups)  14.5 us
    pallas_call x1, Pallas kernels, planes_device(): talk(give_back, shape((rows, channels), half), [VMEM], [], 3, 1, 3)  12 us
    pallas_call x1, Pallas kernels, planes_device(): pl.pallas_call(run_states, out_shape=shape((all_rows, width), half), in_s...  8.54 us
    ppermute x2, starting transfers between devices, passed_along(): lax.ppermute(value, axis, [(source, source + steps) for source in range(l...  7.53 us
    psum x1, blocking collectives, planes_device(): low_rank = lax.psum(partial_value, 'ch').astype(half)  6.12 us
    dot_general x1, matrix products, planes_device(): lax.dot_general(tok_all.reshape(all_rows, channels), pin_all.reshape(GROU...  5.51 us
  transfers between devices with their start and end apart: 2, of which 0 were waited for; matrix products, arithmetic and copies ran while one was open for 8% of the time, Pallas kernels for 13%

profile of v1, /device:TPU:0, one launch (start us, length us, event | category | flops | bytes accessed | tf_op | source)
XLA Modules:
  0.0 199.7 jit_solution(9984536018132577921)
XLA Ops:
  0.0 84.0 %shard_map.91 = (bf16[4,128,4096]{2,1,0:T(8,128)(2,1)}, bf16[4,96,4096]{2,1,0:T(8,128)(2,1)}, bf16[2,96,1024]{2,1,0:T(8,128)(2,1)}, bf16[2,4,96,1024]{3,2,1,0:T(8,128)(2,1)}) custom-call(bf16[128,4096]{1,0:T(8,128)(2,1)} %tok.1, bf16[96,4096]{1,0:T(8,128)(2,1)} %bitcast.71, bf16[96,4096]{1,0:T(8,128)(2,1)} %pout.1), custom_call_target="tpu_custom_call" | custom-call | tf_op jit(solution)/shard_map/pallas_call | solution.py:293
  84.0 5.5 %fusion.29 = f32[512,384]{1,0:T(8,128)S(1)} fusion(bf16[512,4096]{1,0:T(8,128)(2,1)} %bitcast.96, bf16[384,4096]{1,0:T(8,128)(2,1)} %bitcast.97), kind=kOutput, calls=%fused_computation.75 | convolution fusion | flops 1610612736 | bytes 8126464 | tf_op jit(solution)/shard_map/dot_general | solution.py:299
  89.5 6.1 %all-reduce.1.low = bf16[512,384]{1,0:T(8,128)(2,1)} all-reduce(f32[512,384]{1,0:T(8,128)S(1)} %fusion.29), channel_id=1, replica_groups=mesh['seq'=16,'ch'=2] {'ch'}, use_global_device_ids=true, to_apply=%region_0.1 | all-reduce | flops 196608 | bytes 1179648 | tf_op jit(solution)/shard_map/psum | solution.py:302
  95.7 31.9 %shard_map.92 = (bf16[512,1536]{1,0:T(8,128)(2,1)}, bf16[2,4,96,1024]{3,2,1,0:T(8,128)(2,1)}, bf16[4,128,1024]{2,1,0:T(8,128)(2,1)}) custom-call(bf16[512,384]{1,0:T(8,128)(2,1)} %all-reduce.1.low, bf16[2,96,1024]{2,1,0:T(8,128)(2,1)} %get-tuple-element.16.rows, bf16[128,4096]{1,0:T(8,128)(2,1)} %key.1), custom_call_target="tpu_custom_call" | custom-call | tf_op jit(solution)/shard_map/pallas_call | solution.py:303
  127.5 1.8 pad_maximum_fusion
  129.4 1.8 convolution_convert_fusion
  131.9 3.5 %collective-permute-start.1 = (bf16[2,6,1024]{2,1,0:T(8,128)(2,1)}, bf16[2,6,1024]{2,1,0:T(8,128)(2,1)}, u32[]{:S(2)}, u32[]{:S(2)}) collective-permute-start(bf16[2,6,1024]{2,1,0:T(8,128)(2,1)} %pad_maximum_fusion.1), channel_id=1, source_target_pairs={{0,8},{2,10},{4,12},{6,14},{8,16},{10,18},{12,20},{14,22},{16,24},... | collective-permute-start | bytes 73736 | tf_op jit(solution)/shard_map/ppermute | solution.py:369
  135.4 0.6 slice.199
  136.1 4.0 %collective-permute-start = (bf16[6,4096]{1,0:T(8,128)(2,1)}, bf16[6,4096]{1,0:T(8,128)(2,1)}, u32[]{:S(2)}, u32[]{:S(2)}) collective-permute-start(bf16[6,4096]{1,0:T(8,128)(2,1)} %slice.199), channel_id=1, source_target_pairs={{0,2},{2,4},{4,6},{6,8},{8,10},{10,12},{12,14},{14,16},{16,18},{18... | collective-permute-start | bytes 147464 | tf_op jit(solution)/shard_map/ppermute | solution.py:369
  140.1 1.0 slice.213
  141.0 2.1 %fusion.28 = (f32[1,1,4096]{2,1,0:T(1,128)}, f32[1,1,4096]{2,1,0:T(1,128)}, f32[1,1,4096]{2,1,0:T(1,128)}, f32[1,1,4096]{2,1,0:T(1,128)}, f32[1,1,4096]{2,1,0:T(...) fusion(f32[3,7,4096]{2,1,0:T(8,128)} %param.14), kind=kLoop, calls=%fused_computation.74 | loop fusion | bytes 229376 | tf_op jit(solution)/shard_map/slice | solution.py:376
  143.2 1.5 multiply_bitcast_fusion
  144.7 0.8 constant_dynamic-slice_fusion.6
  146.1 1.5 copy.10
  147.6 0.6 copy.12
  148.2 0.7 slice_bitcast_fusion.1
  150.1 4.3 %fusion.2.mixed = bf16[512,1024]{1,0:T(8,128)(2,1)} fusion(f32[518,1024]{1,0:T(8,128)S(1)} %maximum_convert_fusion.2, f32[518,1024]{1,0:T(8,128)S(1)} %maximum_convert_fusion.1, f32[1024]{0:T(1024)S(1)} %bitcast.95, f32[1024]{0:T(1024)S(1)} %bitcast.83, f32[1024]{0:T(1024)S(1)} %bitcast.84, f32[1024]{0:T(1024)S(1)} %bitcast.85, f32[1024]{0:T(1024)S(1)} %bitcast.86, ...), kind=kLoop, calls=%fused_computation.4 | loop fusion | flops 14680064 | bytes 30466048 | tf_op jit(solution)/shard_map/convert_element_type | solution.py:321
  154.4 5.4 %shard_map.93 = (f32[4096,128]{1,0:T(8,128)}, f32[16,8,128]{2,1,0:T(8,128)}) custom-call(bf16[512,1024]{1,0:T(8,128)(2,1)} %fusion.2.mixed, f32[16,8,128]{2,1,0:T(8,128)} %bitcast.72), custom_call_target="tpu_custom_call" | custom-call | tf_op jit(solution)/shard_map/pallas_call | solution.py:326
  159.8 14.5 %all-gather = f32[64,8,128]{2,1,0:T(8,128)S(1)} all-gather(f32[16,8,128]{2,1,0:T(8,128)} %get-tuple-element.22), channel_id=2, replica_groups={{0,8,16,24},{2,10,18,26},{4,12,20,28},{6,14,22,30},{1,9,17,25},{3,11,19..., dimensions={0}, use_global_device_ids=true | all-gather | bytes 327680 | tf_op jit(solution)/shard_map/all_gather | solution.py:333
  174.3 0.6 fusion.27.carried
  175.0 8.5 %shard_map.94.mine = bf16[512,1024]{1,0:T(8,128)(2,1)} custom-call(f32[4096,128]{1,0:T(8,128)} %get-tuple-element.21.spread, f32[16,8,128]{2,1,0:T(8,128)} %fusion.27.carried, f32[16,8,128]{2,1,0:T(8,128)} %bitcast.73, f32[16,8,128]{2,1,0:T(8,128)} %bitcast.74, f32[8,128]{1,0:T(8,128)} %dynamic-slice_bitcast_fusion.skip), custom_call_target="tpu_custom_call" | custom-call | tf_op jit(solution)/shard_map/pallas_call | solution.py:338
  183.5 12.0 %shard_map.95 = bf16[128,4096]{1,0:T(8,128)(2,1)} custom-call(bf16[512,1024]{1,0:T(8,128)(2,1)} %shard_map.94.mine), custom_call_target="tpu_custom_call" | custom-call | tf_op jit(solution)/shard_map/pallas_call | solution.py:344
  195.7 1.2 maximum_convert_fusion
  197.0 2.7 %fusion.16 = bf16[128,4096]{1,0:T(8,128)(2,1)} fusion(f32[134,4096]{1,0:T(8,128)S(1)} %maximum_convert_fusion, bf16[128,4096]{1,0:T(8,128)(2,1)S(1)} %copy-done.1, f32[4096]{0:T(1024)S(1)} %bitcast.81, f32[4096]{0:T(1024)S(1)} %bitcast.76, f32[4096]{0:T(1024)S(1)} %bitcast.77, f32[4096]{0:T(1024)S(1)} %bitcast.78, f32[4096]{0:T(1024)S(1)} %bitcast.79, ...), kind=kLoop, calls=%fused_computation.32 | loop fusion | flops 8388608 | bytes 16891904 | tf_op jit(solution)/shard_map/convert_element_type | solution.py:346
  (62 shorter events, 2.4 us)
Async XLA Ops:
  0.0 145.5 %copy-start = (f32[4096]{0:T(1024)S(1)}, f32[4096]{0:T(1024)}, u32[]{:S(2)}) copy-start(f32[4096]{0:T(1024)} %param.17) | copy-start | bytes 49156
  89.5 38.0 %copy-start.2 = (bf16[2,4,96,1024]{3,2,1,0:T(8,128)(2,1)S(1)}, bf16[2,4,96,1024]{3,2,1,0:T(8,128)(2,1)}, u32[]{:S(2)}) copy-start(bf16[2,4,96,1024]{3,2,1,0:T(8,128)(2,1)} %get-tuple-element.19) | copy-start | bytes 4718596
  127.5 1.9 copy-start.26
  129.4 1.8 copy-start.4
  129.4 6.0 %copy-start.3 = (bf16[128,4096]{1,0:T(8,128)(2,1)S(1)}, bf16[128,4096]{1,0:T(8,128)(2,1)}, u32[]{:S(2)}) copy-start(bf16[128,4096]{1,0:T(8,128)(2,1)} %param.10) | copy-start | bytes 3145732
  131.9 16.4 %collective-permute-start.1 = (bf16[2,6,1024]{2,1,0:T(8,128)(2,1)}, bf16[2,6,1024]{2,1,0:T(8,128)(2,1)}, u32[]{:S(2)}, u32[]{:S(2)}) collective-permute-start(bf16[2,6,1024]{2,1,0:T(8,128)(2,1)} %pad_maximum_fusion.1), channel_id=1, source_target_pairs={{0,8},{2,10},{4,12},{6,14},{8,16},{10,18},{12,20},{14,22},{16,24},... | collective-permute-start | bytes 73736 | tf_op jit(solution)/shard_map/ppermute | solution.py:369
  136.1 59.6 %collective-permute-start = (bf16[6,4096]{1,0:T(8,128)(2,1)}, bf16[6,4096]{1,0:T(8,128)(2,1)}, u32[]{:S(2)}, u32[]{:S(2)}) collective-permute-start(bf16[6,4096]{1,0:T(8,128)(2,1)} %slice.199), channel_id=1, source_target_pairs={{0,2},{2,4},{4,6},{6,8},{8,10},{10,12},{12,14},{14,16},{16,18},{18... | collective-permute-start | bytes 147464 | tf_op jit(solution)/shard_map/ppermute | solution.py:369
  149.3 0.7 copy-start.13
  149.3 0.7 copy-start.14
  149.3 0.7 copy-start.15
  149.4 0.7 copy-start.18
  149.4 0.7 copy-start.20
  149.4 0.7 copy-start.21
  149.4 0.7 copy-start.22
  149.4 0.7 copy-start.23
  149.4 0.7 copy-start.25
  195.6 1.3 copy-start.1
  195.6 1.3 copy-start.5
  195.6 1.3 copy-start.6
  195.6 1.3 copy-start.7
  195.6 1.3 copy-start.8
  195.6 1.3 copy-start.9
  195.6 1.3 copy-start.10
  195.6 1.3 copy-start.11
  (5 other events, 3.4 us)

commit v2 on v1

--- a/solution.py
+++ b/solution.py
@@ -91,98 +91,138 @@
     return copies
 
 
-def gather_first(tok, pin, pout, tok_all, pin_all, rows_late, rows_early, pieces, send, recv, local):
+def multiple(value, by):
+    return pl.multiple_of(value, by)
+
+
+def fetch_all(
+    tok, pin, pout, key, query_tail, low_all, rows_all, key_all, query_edge,
+    tok_all, pin_all, pieces, key_more, partial, inbox, low, send, recv, local,
+):
     plane, spot, flat, tall = rings()
+    core = lax.axis_index("ch")
+    me, count = lax.axis_index("seq"), lax.axis_size("seq")
     sems = (send, recv)
-    width = pieces.shape[-1]
-    greet(everyone(plane, spot, tall))
-
-    def piece(peer):
-        return pout.at[:, pl.ds(pl.multiple_of(peer * width, width), width)]
-
-    half_tok, half_pin = tok.shape[0] // 2, pin.shape[0] // 2
-    moved = swap(piece, lambda s: pieces.at[s], sems, 18, plane, spot)
-    for copy in moved:
-        copy.start()
+    rows, ranks, width = tok.shape[0], pin.shape[0], pieces.shape[-1]
+    margin = query_tail.shape[0]
+    after, before = {"seq": (me + 1) % count}, {"seq": (me + count - 1) % count}
+    partner = {"ch": 1 - core}
+    greet(everyone(plane, spot, tall) + [partner, after, before])
+
+    def columns(s, extent):
+        return pl.ds(multiple(s * extent, extent), extent)
+
+    half_tok, half_pin, half_low = rows // 2, ranks // 2, low.shape[0] // 2
+
+    def low_rows(h):
+        return pl.ds(multiple(margin + core * low.shape[0] + h * half_low, 16), half_low)
+
+    tails = [
+        remote(key.at[pl.ds(rows - margin, margin)], key_more.at[pl.ds(0, margin)], sems, 0, after),
+        remote(query_tail, query_edge, sems, 1, after),
+    ]
+    rank_swap = swap(
+        lambda peer: pout.at[:, columns(peer, width)], lambda s: pieces.at[s], sems, 2, plane, spot)
+    key_swap = swap(
+        lambda peer: key_more.at[:, columns(peer, width)], lambda s: key_all.at[s], sems, 5,
+        plane, spot)
     tokens_ring = Ring(
         lambda h: tok.at[pl.ds(h * half_tok, half_tok)],
-        lambda s, h: tok_all.at[s, pl.ds(h * half_tok, half_tok)], sems, 0, *flat)
+        lambda s, h: tok_all.at[s, pl.ds(h * half_tok, half_tok)], sems, 8, *flat)
     pin_ring = Ring(
         lambda h: pin.at[pl.ds(h * half_pin, half_pin)],
-        lambda s, h: pin_all.at[s, pl.ds(h * half_pin, half_pin)], sems, 6, *tall)
+        lambda s, h: pin_all.at[pl.ds(multiple(s * ranks + h * half_pin, 16), half_pin)],
+        sems, 14, *tall)
+    rows_ring = Ring(
+        lambda h: pieces.at[pl.ds(h * 2, 2)], lambda s, h: rows_all.at[pl.ds(h * 2, 2), s],
+        sems, 20, *tall)
+    low_ring = Ring(
+        lambda h: low.at[pl.ds(h * half_low, half_low)],
+        lambda s, h: low_all.at[low_rows(h), columns(s, low.shape[1])], sems, 26, *flat)
+    mine = pl.ds(multiple(core * low.shape[0], 16), low.shape[0])
+    others = pl.ds(multiple((1 - core) * low.shape[0], 16), low.shape[0])
+    sums = remote(partial.at[others], inbox, sems, 32, partner)
+    my_low = low_all.at[pl.ds(multiple(margin + core * low.shape[0], 16), low.shape[0])]
+    lows = remote(my_low, my_low, sems, 33, partner)
+    edge = remote(
+        low_all.at[pl.ds(low_all.shape[0] - margin, margin)], low_all.at[pl.ds(0, margin)],
+        sems, 34, tall[4])
+
+    pin_ring.start()
+    for copy in rank_swap + tails:
+        copy.start()
     tokens_ring.start()
-    pin_ring.start()
     keep = [
         pltpu.make_async_copy(tok, tok_all.at[spot], local.at[0]),
-        pltpu.make_async_copy(pin, pin_all.at[plane], local.at[1]),
-        pltpu.make_async_copy(piece(spot), pieces.at[spot], local.at[2]),
+        pltpu.make_async_copy(pin, pin_all.at[columns(plane, ranks)], local.at[1]),
+        pltpu.make_async_copy(pout.at[:, columns(spot, width)], pieces.at[spot], local.at[2]),
+        pltpu.make_async_copy(key, key_more.at[pl.ds(margin, rows)], local.at[3]),
     ]
     for copy in keep:
         copy.start()
+    for copy in keep:
+        copy.wait()
+    for copy in tails:
+        copy.wait_recv()
     pin_ring.relay()
-    keep[2].wait()
-    for copy in moved:
+    for copy in rank_swap:
         copy.wait_recv()
-    rows_ring = Ring(
-        lambda h: pieces.at[h], lambda s, h: rows_early.at[h, s], sems, 12, *tall)
     rows_ring.start()
     last = [
-        pltpu.make_async_copy(pieces.at[pl.ds(2, 2)], rows_late, local.at[3]),
-        pltpu.make_async_copy(pieces.at[0], rows_early.at[0, plane], local.at[4]),
-        pltpu.make_async_copy(pieces.at[1], rows_early.at[1, plane], local.at[5]),
+        pltpu.make_async_copy(pieces, rows_all.at[:, plane], local.at[4]),
+        pltpu.make_async_copy(key_more.at[:, columns(spot, width)], key_all.at[spot], local.at[5]),
     ]
     for copy in last:
         copy.start()
     tokens_ring.relay()
-    rows_ring.relay()
+    for copy in key_swap:
+        copy.start()
+    tokens_ring.finish()
     pin_ring.finish()
-    tokens_ring.finish()
-    rows_ring.finish()
-    for copy in moved:
-        copy.wait_send()
-    for copy in keep[:2] + last:
-        copy.wait()
-
-
-def gather_second(low, rows, key, low_all, rows_all, key_all, send, recv, local):
-    plane, spot, flat, tall = rings()
-    sems = (send, recv)
-    width, ranks, half = key_all.shape[-1], low.shape[1], low.shape[0] // 2
-    greet(everyone(plane, spot, tall))
-
-    def columns(s):
-        return pl.ds(pl.multiple_of(s * ranks, ranks), ranks)
-
-    def piece(peer):
-        return key.at[:, pl.ds(pl.multiple_of(peer * width, width), width)]
-
-    low_ring = Ring(
-        lambda h: low.at[pl.ds(h * half, half)],
-        lambda s, h: low_all.at[pl.ds(h * half, half), columns(s)], sems, 0, *flat)
-    rows_ring = Ring(lambda h: rows.at[h], lambda s, h: rows_all.at[h, s], sems, 6, *tall)
-    moved = swap(piece, lambda s: key_all.at[s], sems, 12, plane, spot)
+
+    @pl.loop(0, GROUP)
+    def _(s):
+        partial[pl.ds(multiple(s * rows, rows), rows), :] = lax.dot_general(
+            tok_all[s], pin_all[...], (((1,), (1,)), ((), ())),
+            preferred_element_type=jnp.float32)
+
+    sums.start()
+    sums.wait()
+    low[...] = (partial[mine, :] + inbox[...]).astype(low.dtype)
     low_ring.start()
-    rows_ring.start()
-    keep = [
-        pltpu.make_async_copy(low, low_all.at[:, columns(spot)], local.at[0]),
-        pltpu.make_async_copy(rows.at[0], rows_all.at[0, plane], local.at[1]),
-        pltpu.make_async_copy(rows.at[1], rows_all.at[1, plane], local.at[2]),
-        pltpu.make_async_copy(piece(spot), key_all.at[spot], local.at[3]),
-    ]
-    for copy in keep:
-        copy.start()
+    keep_low = pltpu.make_async_copy(low, my_low.at[:, columns(spot, low.shape[1])], local.at[6])
+    keep_low.start()
     low_ring.relay()
-    for copy in moved:
-        copy.start()
     rows_ring.relay()
     low_ring.finish()
+    keep_low.wait()
+    lows.start()
+    lows.wait()
+    edge.start()
+    for copy in key_swap:
+        copy.wait_recv()
     rows_ring.finish()
-    for copy in moved:
-        copy.wait_recv()
-    for copy in moved:
+    edge.wait()
+    for copy in rank_swap + key_swap + tails:
         copy.wait_send()
-    for copy in keep:
+    for copy in last:
         copy.wait()
+
+
+def share_states(mine, ends, send, recv, local):
+    plane, spot = where_am_i()
+    peers = [device((plane + step) % GROUP, spot) for step in range(1, GROUP)]
+    greet(peers)
+    copies = [
+        remote(mine, ends.at[plane], (send, recv), index, peer) for index, peer in enumerate(peers)
+    ]
+    for copy in copies:
+        copy.start()
+    keep = pltpu.make_async_copy(mine, ends.at[plane], local.at[0])
+    keep.start()
+    for copy in copies:
+        copy.wait()
+    keep.wait()
 
 
 def give_back(mine, out, send, recv, local):
@@ -224,30 +264,64 @@
     )
 
 
-def end_states(mixed, decay, spread, states):
-    rows, (modes, tall, lanes) = mixed.shape[0], decay.shape
-
-    @pl.loop(0, rows // 16)
+def end_states(value, key, taps, decay, live, spread, states, values, keys):
+    modes, tall, lanes = decay.shape
+    margin = value.shape[0] - spread.shape[0] // tall
+    count, rows = taps.shape[1], spread.shape[0] // tall
+    piece = key.shape[1] - margin
+
+    def lay(target, start, load):
+        for column in range(tall):
+            tile = load(slice(column * lanes, (column + 1) * lanes)).astype(jnp.float32)
+            target[pl.ds(start * tall + column, 16, stride=tall), :] = tile
+
+    @pl.loop(0, value.shape[0] // 16)
     def _(block):
         start = pl.multiple_of(block * 16, 16)
-        for column in range(tall):
-            tile = mixed[pl.ds(start, 16), column * lanes:(column + 1) * lanes]
-            spread[pl.ds(start * tall + column, 16, stride=tall), :] = tile.astype(jnp.float32)
+        lay(values, start, lambda cols: value[pl.ds(start, 16), cols])
+
+    for edge in range(0, margin, 16):
+        lay(keys, edge, lambda cols: key[0, edge:edge + 16, cols])
+    for part in range(key.shape[0]):
+
+        @pl.loop(0, piece // 16)
+        def _(block):
+            start = pl.multiple_of(block * 16, 16)
+            lay(keys, margin + part * piece + start,
+                lambda cols: key[part, pl.ds(margin + start, 16), cols])
+
+    on = live[...]
+    for row in range(margin):
+        for target in (values, keys):
+            place = slice(row * tall, (row + 1) * tall)
+            target[place, :] = target[place, :] * on
 
     rates = [decay[mode] for mode in range(modes)]
+    gains = [[taps[branch, tap] for tap in range(count)] for branch in range(2)]
+
+    def short(source, gain, at):
+        total = None
+        for tap in range(count):
+            place = pl.ds(pl.multiple_of((at + margin - tap) * tall, tall), tall)
+            term = gain[tap] * source[place, :]
+            total = term if total is None else total + term
+        return total
 
     def step(at, held):
-        for part in range(8):
-            value = spread[pl.ds(pl.multiple_of((at * 8 + part) * tall, tall), tall), :]
-            held = [h * r + value for h, r in zip(held, rates)]
+        for part in range(4):
+            now = at * 4 + part
+            mixed = short(keys, gains[0], now) * short(values, gains[1], now)
+            mixed = mixed.astype(jnp.bfloat16).astype(jnp.float32)
+            spread[pl.ds(pl.multiple_of(now * tall, tall), tall), :] = mixed
+            held = [h * r + mixed for h, r in zip(held, rates)]
         return held
 
-    held = lax.fori_loop(0, rows // 8, step, [jnp.zeros((tall, lanes), jnp.float32)] * modes)
+    held = lax.fori_loop(0, rows // 4, step, [jnp.zeros((tall, lanes), jnp.float32)] * modes)
     for mode in range(modes):
         states[mode] = held[mode]
 
 
-def run_states(spread, carried, decay, weight, skip, out, kept):
+def run_states(spread, ends, earlier, block, decay, weight, skip, out, kept):
     modes, tall, lanes = decay.shape
     rows = out.shape[0]
     rates = [decay[mode] for mode in range(modes)]
@@ -266,7 +340,13 @@
             kept[place, :] = rounded + gain * value
         return held
 
-    lax.fori_loop(0, rows // 4, step, [carried[mode] for mode in range(modes)])
+    carried = []
+    for mode in range(modes):
+        total = jnp.zeros((tall, lanes), jnp.float32)
+        for at in range(ends.shape[0] - 1):
+            total = jnp.where(earlier[at] > 0, total * block[mode] + ends[at, mode], total)
+        carried.append(total)
+    lax.fori_loop(0, rows // 4, step, carried)
 
     @pl.loop(0, rows // 16)
     def _(block):
@@ -288,60 +368,50 @@
     half = jnp.bfloat16
     shape = jax.ShapeDtypeStruct
     plane, spot = where_am_i()
-    query_previous = passed_along(query_in[rows - margin_rows:], "seq", 1)
-
-    tok_all, pin_all, late, early = talk(
-        gather_first,
-        [shape((GROUP, rows, channels), half), shape((GROUP, ranks, channels), half),
-         shape((2, ranks, width), half), shape((2, GROUP, ranks, width), half)],
-        [VMEM] * 3, [pltpu.VMEM((GROUP, ranks, width), half)], 21, 6, 1,
-    )(tokens, proj_in.T, proj_out)
-    partial_value = lax.dot_general(
-        tok_all.reshape(all_rows, channels), pin_all.reshape(GROUP * ranks, channels),
-        (((1,), (1,)), ((), ())), preferred_element_type=jnp.float32)
-    low_rank = lax.psum(partial_value, "ch").astype(half)
-    low_all, rest, key_all = talk(
-        gather_second,
-        [shape((all_rows, GROUP * GROUP * ranks), half), shape((2, GROUP, ranks, width), half),
-         shape((GROUP, rows, width), half)],
-        [VMEM] * 3, [], 15, 4, 2,
-    )(low_rank, late, key_in)
-    factor = jnp.concatenate([early, rest], axis=0).reshape(GROUP * GROUP * ranks, width)
-    value = jnp.dot(low_all, factor, preferred_element_type=jnp.float32).astype(half)
-    key = key_all.reshape(all_rows, width)
+    margin = 16
+    share, both = GROUP * ranks, GROUP * GROUP * ranks
+
+    low_all, rows_all, key_all, query_edge = talk(
+        fetch_all,
+        [shape((margin + all_rows, both), half), shape((GROUP, GROUP, ranks, width), half),
+         shape((GROUP, margin + rows, width), half), shape((margin, channels), half)],
+        [VMEM] * 5,
+        [pltpu.VMEM((GROUP, rows, channels), half), pltpu.VMEM((share, channels), half),
+         pltpu.VMEM((GROUP, ranks, width), half), pltpu.VMEM((margin + rows, channels), half),
+         pltpu.VMEM((all_rows, share), jnp.float32),
+         pltpu.VMEM((all_rows // 2, share), jnp.float32), pltpu.VMEM((all_rows // 2, share), half)],
+        35, 7, 1,
+    )(tokens, proj_in.T, proj_out, key_in, query_in[rows - margin:])
+    value = jnp.dot(
+        low_all, rows_all.reshape(both, width), preferred_element_type=jnp.float32).astype(half)
 
     def mine(part):
         return lax.dynamic_slice_in_dim(part, spot * width, width, part.ndim - 1)
 
-    taps, rates, weights = mine(short_taps[1:]), mine(mode_rates), mine(residues)
-    edges = passed_along(
-        jnp.stack([key[all_rows - margin_rows:], value[all_rows - margin_rows:]]), "seq", GROUP)
-    mixed = (
-        short_filter(edges[0], key, taps[0]) * short_filter(edges[1], value, taps[1])
-    ).astype(half)
-    tiles = (modes, tall, 128)
+    tiles, tile = (modes, tall, 128), (tall, 128)
+    rates, weights = mine(mode_rates), mine(residues)
     weights = (weights * jnp.sqrt(rates)).reshape(tiles)
     rates = rates.reshape(tiles)
-    decay = jnp.exp(-rates)
+    decay, block = jnp.exp(-rates), jnp.exp(-rates * all_rows)
+    taps = mine(short_taps[1:]).reshape(2, margin_rows + 1, *tile)
+    order = jnp.arange(GROUP - 1)[:, None, None]
+    earlier = jnp.broadcast_to((order < plane).astype(jnp.float32), (GROUP - 1, *tile))
+    scattered = pltpu.VMEM(((margin + all_rows) * tall, 128), jnp.float32)
     spread, states = pl.pallas_call(
         end_states,
         out_shape=[shape((all_rows * tall, 128), jnp.float32), shape(tiles, jnp.float32)],
-        in_specs=[VMEM] * 2, out_specs=[VMEM] * 2,
-    )(mixed, decay)
-    count = lax.axis_size("seq") // GROUP
-    groups = [[at * GROUP + s for at in range(count)] for s in range(GROUP)]
-    ends = lax.all_gather(states, "seq", axis_index_groups=groups)
-    carried = jnp.zeros(tiles, jnp.float32)
-    block = jnp.exp(-rates * all_rows)
-    for at in range(count - 1):
-        carried = jnp.where(at < plane, carried * block + ends[at], carried)
+        in_specs=[VMEM] * 5, out_specs=[VMEM] * 2, scratch_shapes=[scattered, scattered],
+    )(value, key_all, taps, decay, earlier[0])
+    ends = talk(share_states, shape((GROUP, *tiles), jnp.float32), [VMEM], [], 3, 1, 2)(states)
     mixed_out = pl.pallas_call(
         run_states,
         out_shape=shape((all_rows, width), half),
-        in_specs=[VMEM] * 5, out_specs=VMEM,
+        in_specs=[VMEM] * 7, out_specs=VMEM,
         scratch_shapes=[pltpu.VMEM((all_rows * tall, 128), jnp.float32)],
-    )(spread, carried, decay, weights, mine(skip_gain).reshape(tall, 128))
+    )(spread, ends, earlier, block, decay, weights, mine(skip_gain).reshape(tile))
     given = talk(give_back, shape((rows, channels), half), [VMEM], [], 3, 1, 3)(mixed_out)
+    first = lax.axis_index("seq") == 0
+    query_previous = jnp.where(first, 0, query_edge[margin - margin_rows:]).astype(half)
     query_short = short_filter(query_previous, query_in, short_taps[0])
     return (query_short * given.astype(jnp.float32)).astype(half)
 
@@ -457,9 +527,10 @@
     def run(*args):
         rows, channels = args[0].shape
         ranks = args[3].shape[1]
-        square = mesh.shape["seq"] == GROUP * GROUP
+        square = mesh.shape["seq"] == GROUP * GROUP and mesh.shape["ch"] == 2
         whole = channels % (GROUP * 1024) == 0 and ranks % 32 == 0 and rows % 32 == 0
         fits = (GROUP * ranks) % 128 == 0 and channels == GROUP * 1024
+        fits = fits and args[5].shape[1] <= 16
         return (planes_device if square and whole and fits else per_device)(*args)
 
     return run

time: 200 us -> 177 us (0.89)
  blocking collectives: 20.6 us -> 0 us
  Pallas kernels: 142 us -> 159 us
  other arithmetic: 13.5 us -> 3.92 us
  starting transfers between devices: 7.53 us -> 0 us
  matrix products: 7.3 us -> 5.22 us
    all_gather x1 -> x0, blocking collectives: 14.5 us -> none  [planes_device(): ends = lax.all_gather(states, 'seq', axis_index_groups=groups)]
    pallas_call x2, Pallas kernels: 116 us -> 129 us  [the longest x1 120 us: planes_device(): talk(fetch_all, [shape((margin + all_rows, both), half), shape((GROUP, GR...]
    ppermute x2 -> x0, starting transfers between devices: 7.53 us -> none  [passed_along(): lax.ppermute(value, axis, [(source, source + steps) for source in range(l...]
    psum x1 -> x0, blocking collectives: 6.12 us -> none  [planes_device(): low_rank = lax.psum(partial_value, 'ch').astype(half)]
    convert_element_type x1, other arithmetic: 4.33 us -> 0.01 us  [planes_device(): (order < plane).astype(jnp.float32)]
    pallas_call x1, Pallas kernels: 5.39 us -> 9.1 us  [planes_device(): pl.pallas_call(end_states, out_shape=[shape((all_rows * tall, 128), jnp.f...]
    dot_general x2 -> x1, matrix products: 7.3 us -> 5.22 us  [planes_device(): jnp.dot(low_all, rows_all.reshape(both, width), preferred_element_type=jn...]
  transfers between devices with their start and end apart: 2 -> 0, of which waited for: 0 -> 0; matrix products, arithmetic and copies ran while one was open for 8% -> 0% of each run, Pallas kernels for 13% -> 0%
where the time goes in v2:
time: 177 us; the launch traced here: 176 us
  Pallas kernels  159 us (90%)
  local copies, waits for them, and re-layouts  8.48 us (5%)
  matrix products  5.22 us (3%)
  other arithmetic  3.92 us (2%)
    pallas_call x1, Pallas kernels, planes_device(): talk(fetch_all, [shape((margin + all_rows, both), half), shape((GROUP, GR...  120 us
    pallas_call x1, Pallas kernels, planes_device(): talk(give_back, shape((rows, channels), half), [VMEM], [], 3, 1, 3)  11.9 us
    pallas_call x1, Pallas kernels, planes_device(): pl.pallas_call(end_states, out_shape=[shape((all_rows * tall, 128), jnp.f...  9.1 us
    pallas_call x1, Pallas kernels, planes_device(): talk(share_states, shape((GROUP, *tiles), jnp.float32), [VMEM], [], 3, 1, 2)  8.75 us
    pallas_call x1, Pallas kernels, planes_device(): pl.pallas_call(run_states, out_shape=shape((all_rows, width), half), in_s...  8.73 us
    dot_general x1, matrix products, planes_device(): jnp.dot(low_all, rows_all.reshape(both, width), preferred_element_type=jn...  5.22 us

profile of v2, /device:TPU:0, one launch (start us, length us, event | category | flops | bytes accessed | tf_op | source)
XLA Modules:
  0.0 176.4 jit_solution(5943690320476151614)
XLA Ops:
  0.0 0.0 copy-start
  0.0 1.0 slice.88
  1.0 0.6 reshape.50.taps
  1.6 0.9 multiply_bitcast_fusion
  2.6 0.7 copy.10
  3.2 0.6 broadcast_in_dim.19.live
  3.8 1.6 slice.73.query_tail
  5.4 120.2 %shard_map.91 = (bf16[528,1536]{1,0:T(8,128)(2,1)}, bf16[4,4,96,1024]{3,2,1,0:T(8,128)(2,1)}, bf16[4,144,1024]{2,1,0:T(8,128)(2,1)}, bf16[16,4096]{1,0:T(8,128)(2,1)}) custom-call(bf16[128,4096]{1,0:T(8,128)(2,1)} %tok.1, bf16[96,4096]{1,0:T(8,128)(2,1)} %bitcast.24, bf16[96,4096]{1,0:T(8,128)(2,1)} %pout.1, bf16[128,4096]{1,0:T(8,128)(2,1)} %key.1, ...), custom_call_target="tpu_custom_call" | custom-call | tf_op jit(solution)/shard_map/pallas_call | solution.py:374
  125.6 5.2 %convolution_convert_fusion.value = bf16[528,1024]{1,0:T(8,128)(2,1)} fusion(bf16[528,1536]{1,0:T(8,128)(2,1)} %get-tuple-element.12, bf16[1536,1024]{1,0:T(8,128)(2,1)} %bitcast.36), kind=kOutput, calls=%fused_computation.15 | convolution fusion | flops 1661485056 | bytes 5849088 | tf_op jit(solution)/shard_map/dot_general | solution.py:385
  130.8 9.1 %shard_map.92 = (f32[4096,128]{1,0:T(8,128)}, f32[16,8,128]{2,1,0:T(8,128)}) custom-call(bf16[528,1024]{1,0:T(8,128)(2,1)} %convolution_convert_fusion.value, bf16[4,144,1024]{2,1,0:T(8,128)(2,1)} %get-tuple-element.14.key, f32[2,7,8,128]{3,2,1,0:T(8,128)} %reshape.50.taps, f32[16,8,128]{2,1,0:T(8,128)} %bitcast.25, f32[8,128]{1,0:T(8,128)} %broadcast_in_dim.19.live), custom_call_target="tpu_custom_call" | custom-call | tf_op jit(solution)/shard_map/pallas_call | solution.py:400
  139.9 8.8 %shard_map.93.ends = f32[4,16,8,128]{3,2,1,0:T(8,128)} custom-call(f32[16,8,128]{2,1,0:T(8,128)} %get-tuple-element.16.mine), custom_call_target="tpu_custom_call" | custom-call | tf_op jit(solution)/shard_map/pallas_call | solution.py:405
  148.6 0.6 copy.11
  149.3 0.6 copy.12
  149.9 0.0 copy-done
  149.9 0.6 dynamic-slice_bitcast_fusion.skip
  150.5 0.7 broadcast_in_dim.20.earlier
  151.2 8.7 %shard_map.94.mine = bf16[512,1024]{1,0:T(8,128)(2,1)} custom-call(f32[4096,128]{1,0:T(8,128)} %get-tuple-element.15.spread, f32[4,16,8,128]{3,2,1,0:T(8,128)} %shard_map.93.ends, f32[3,8,128]{2,1,0:T(8,128)} %broadcast_in_dim.20.earlier, f32[16,8,128]{2,1,0:T(8,128)} %bitcast.27, f32[16,8,128]{2,1,0:T(8,128)} %bitcast.26, f32[16,8,128]{2,1,0:T(8,128)} %bitcast.28, ...), custom_call_target="tpu_custom_call" | custom-call | tf_op jit(solution)/shard_map/pallas_call | solution.py:406
  159.9 11.9 %shard_map.95 = bf16[128,4096]{1,0:T(8,128)(2,1)} custom-call(bf16[512,1024]{1,0:T(8,128)(2,1)} %shard_map.94.mine), custom_call_target="tpu_custom_call" | custom-call | tf_op jit(solution)/shard_map/pallas_call | solution.py:412
  171.8 0.0 copy-start.1
  171.8 0.0 copy-done.3
  171.9 0.3 maximum_convert_fusion
  172.2 1.5 fusion.8
  173.7 0.0 copy-done.1
  173.7 2.7 %fusion.2 = bf16[128,4096]{1,0:T(8,128)(2,1)} fusion(f32[134,4096]{1,0:T(8,128)S(1)} %maximum_convert_fusion, bf16[128,4096]{1,0:T(8,128)(2,1)S(1)} %copy-done.1, f32[4096]{0:T(1024)S(1)} %bitcast.35, f32[4096]{0:T(1024)S(1)} %bitcast.30, f32[4096]{0:T(1024)S(1)} %bitcast.31, f32[4096]{0:T(1024)S(1)} %bitcast.32, f32[4096]{0:T(1024)S(1)} %bitcast.33, ...), kind=kLoop, calls=%fused_computation.3 | loop fusion | flops 8388608 | bytes 16891904 | tf_op jit(solution)/shard_map/convert_element_type | solution.py:416
  (7 shorter events, 0.0 us)
Async XLA Ops:
  0.0 149.9 %copy-start = (f32[4096]{0:T(1024)S(1)}, f32[4096]{0:T(1024)}, u32[]{:S(2)}) copy-start(f32[4096]{0:T(1024)} %param.17) | copy-start | bytes 49156
  151.2 20.7 %copy-start.3 = (bf16[16,4096]{1,0:T(8,128)(2,1)S(1)}, bf16[16,4096]{1,0:T(8,128)(2,1)}, u32[]{:S(2)}) copy-start(bf16[16,4096]{1,0:T(8,128)(2,1)} %get-tuple-element.11) | copy-start | bytes 393220
  151.2 20.7 %copy-start.2 = (bf16[128,4096]{1,0:T(8,128)(2,1)S(1)}, bf16[128,4096]{1,0:T(8,128)(2,1)}, u32[]{:S(2)}) copy-start(bf16[128,4096]{1,0:T(8,128)(2,1)} %param.10) | copy-start | bytes 3145732
  171.8 1.9 %copy-start.1 = (bf16[128,4096]{1,0:T(8,128)(2,1)S(1)}, bf16[128,4096]{1,0:T(8,128)(2,1)}, u32[]{:S(2)}) copy-start(bf16[128,4096]{1,0:T(8,128)(2,1)} %shard_map.95) | copy-start | bytes 3145732

commit v3 on v2

--- a/solution.py
+++ b/solution.py
@@ -69,6 +69,42 @@
             copy.wait_send()
 
 
+class Line:
+    def __init__(self, own, slot, sems, base, plane, below, above, below_dev, above_dev):
+        last = GROUP - 1
+
+        def block(away):
+            return slot((plane + away + GROUP) % GROUP)
+
+        self.own, self.sent, self.arriving = [], [], []
+        for step in range(last):
+            for side, device_on, ahead in ((1, above_dev, plane < last), (-1, below_dev, plane > 0)):
+                index = base + step + (0 if side > 0 else last)
+                held = plane >= step if side > 0 else plane <= last - step
+                due = plane >= step + 1 if side > 0 else plane <= last - step - 1
+                out = remote(
+                    own if step == 0 else block(-side * step), block(-side * step), sems, index,
+                    device_on)
+                came = block(-side * (step + 1))
+                self.sent.append((ahead & held, out))
+                self.arriving.append((due, remote(came, came, sems, index, device_on)))
+
+    def start(self):
+        for when, copy in self.sent[:2]:
+            pl.when(when)(copy.start)
+
+    def relay(self):
+        for (due, arrived), (when, onward) in zip(self.arriving, self.sent[2:]):
+            pl.when(due)(arrived.wait_recv)
+            pl.when(when)(onward.start)
+
+    def finish(self):
+        for due, arrived in self.arriving[len(self.sent) - 2:]:
+            pl.when(due)(arrived.wait_recv)
+        for when, copy in self.sent:
+            pl.when(when)(copy.wait_send)
+
+
 def rings():
     plane, spot = where_am_i()
     turn = flip(spot)
@@ -96,7 +132,7 @@
 
 
 def fetch_all(
-    tok, pin, pout, key, query_tail, low_all, rows_all, key_all, query_edge,
+    tok, pin, pout, key, query, low_all, rows_all, key_all, query_edge,
     tok_all, pin_all, pieces, key_more, partial, inbox, low, send, recv, local,
 ):
     plane, spot, flat, tall = rings()
@@ -104,7 +140,7 @@
     me, count = lax.axis_index("seq"), lax.axis_size("seq")
     sems = (send, recv)
     rows, ranks, width = tok.shape[0], pin.shape[0], pieces.shape[-1]
-    margin = query_tail.shape[0]
+    margin = query_edge.shape[0]
     after, before = {"seq": (me + 1) % count}, {"seq": (me + count - 1) % count}
     partner = {"ch": 1 - core}
     greet(everyone(plane, spot, tall) + [partner, after, before])
@@ -112,14 +148,14 @@
     def columns(s, extent):
         return pl.ds(multiple(s * extent, extent), extent)
 
-    half_tok, half_pin, half_low = rows // 2, ranks // 2, low.shape[0] // 2
+    half_tok, half_low = rows // 2, low.shape[0] // 2
 
     def low_rows(h):
         return pl.ds(multiple(margin + core * low.shape[0] + h * half_low, 16), half_low)
 
     tails = [
         remote(key.at[pl.ds(rows - margin, margin)], key_more.at[pl.ds(0, margin)], sems, 0, after),
-        remote(query_tail, query_edge, sems, 1, after),
+        remote(query.at[pl.ds(rows - margin, margin)], query_edge, sems, 1, after),
     ]
     rank_swap = swap(
         lambda peer: pout.at[:, columns(peer, width)], lambda s: pieces.at[s], sems, 2, plane, spot)
@@ -129,13 +165,9 @@
     tokens_ring = Ring(
         lambda h: tok.at[pl.ds(h * half_tok, half_tok)],
         lambda s, h: tok_all.at[s, pl.ds(h * half_tok, half_tok)], sems, 8, *flat)
-    pin_ring = Ring(
-        lambda h: pin.at[pl.ds(h * half_pin, half_pin)],
-        lambda s, h: pin_all.at[pl.ds(multiple(s * ranks + h * half_pin, 16), half_pin)],
-        sems, 14, *tall)
-    rows_ring = Ring(
-        lambda h: pieces.at[pl.ds(h * 2, 2)], lambda s, h: rows_all.at[pl.ds(h * 2, 2), s],
-        sems, 20, *tall)
+    pin_ring = Line(
+        pin, lambda s: pin_all.at[columns(s, ranks)], sems, 14, *tall)
+    rows_ring = Line(pieces, lambda s: rows_all.at[:, s], sems, 20, *tall)
     low_ring = Ring(
         lambda h: low.at[pl.ds(h * half_low, half_low)],
         lambda s, h: low_all.at[low_rows(h), columns(s, low.shape[1])], sems, 26, *flat)
@@ -375,13 +407,13 @@
         fetch_all,
         [shape((margin + all_rows, both), half), shape((GROUP, GROUP, ranks, width), half),
          shape((GROUP, margin + rows, width), half), shape((margin, channels), half)],
-        [VMEM] * 5,
+        [VMEM] * 4 + [ANY],
         [pltpu.VMEM((GROUP, rows, channels), half), pltpu.VMEM((share, channels), half),
          pltpu.VMEM((GROUP, ranks, width), half), pltpu.VMEM((margin + rows, channels), half),
          pltpu.VMEM((all_rows, share), jnp.float32),
          pltpu.VMEM((all_rows // 2, share), jnp.float32), pltpu.VMEM((all_rows // 2, share), half)],
         35, 7, 1,
-    )(tokens, proj_in.T, proj_out, key_in, query_in[rows - margin:])
+    )(tokens, proj_in.T, proj_out, key_in, query_in)
     value = jnp.dot(
         low_all, rows_all.reshape(both, width), preferred_element_type=jnp.float32).astype(half)
 

time: 177 us -> 175 us (0.989)
  no operation moved by 1% of the time
where the time goes in v3:
time: 175 us
  Pallas kernels  159 us (91%)
  local copies, waits for them, and re-layouts  6.92 us (4%)
  matrix products  5.21 us (3%)
  other arithmetic  3.92 us (2%)
    pallas_call x1, Pallas kernels, planes_device(): talk(fetch_all, [shape((margin + all_rows, both), half), shape((GROUP, GR...  120 us
    pallas_call x1, Pallas kernels, planes_device(): talk(give_back, shape((rows, channels), half), [VMEM], [], 3, 1, 3)  12.8 us
    pallas_call x1, Pallas kernels, planes_device(): pl.pallas_call(end_states, out_shape=[shape((all_rows * tall, 128), jnp.f...  9.1 us
    pallas_call x1, Pallas kernels, planes_device(): pl.pallas_call(run_states, out_shape=shape((all_rows, width), half), in_s...  8.73 us
    pallas_call x1, Pallas kernels, planes_device(): talk(share_states, shape((GROUP, *tiles), jnp.float32), [VMEM], [], 3, 1, 2)  8 us
    dot_general x1, matrix products, planes_device(): jnp.dot(low_all, rows_all.reshape(both, width), preferred_element_type=jn...  5.21 us

profile of v3, /device:TPU:0, one launch (start us, length us, event | category | flops | bytes accessed | tf_op | source)
XLA Modules:
  0.0 175.0 jit_solution(13785908218185640491)
XLA Ops:
  0.0 0.0 copy-start
  0.0 1.0 slice.84
  1.0 0.6 reshape.50.taps
  1.6 0.9 multiply_bitcast_fusion
  2.6 0.7 copy.10
  3.2 0.6 broadcast_in_dim.19.live
  3.8 120.2 %shard_map.91 = (bf16[528,1536]{1,0:T(8,128)(2,1)}, bf16[4,4,96,1024]{3,2,1,0:T(8,128)(2,1)}, bf16[4,144,1024]{2,1,0:T(8,128)(2,1)}, bf16[16,4096]{1,0:T(8,128)(2,1)}) custom-call(bf16[128,4096]{1,0:T(8,128)(2,1)} %tok.1, bf16[96,4096]{1,0:T(8,128)(2,1)} %bitcast.24, bf16[96,4096]{1,0:T(8,128)(2,1)} %pout.1, bf16[128,4096]{1,0:T(8,128)(2,1)} %key.1, ...), custom_call_target="tpu_custom_call" | custom-call | tf_op jit(solution)/shard_map/pallas_call | solution.py:406
  124.0 5.2 %convolution_convert_fusion.value = bf16[528,1024]{1,0:T(8,128)(2,1)} fusion(bf16[528,1536]{1,0:T(8,128)(2,1)} %get-tuple-element.12, bf16[1536,1024]{1,0:T(8,128)(2,1)} %bitcast.36), kind=kOutput, calls=%fused_computation.15 | convolution fusion | flops 1661485056 | bytes 5849088 | tf_op jit(solution)/shard_map/dot_general | solution.py:417
  129.2 9.1 %shard_map.92 = (f32[4096,128]{1,0:T(8,128)}, f32[16,8,128]{2,1,0:T(8,128)}) custom-call(bf16[528,1024]{1,0:T(8,128)(2,1)} %convolution_convert_fusion.value, bf16[4,144,1024]{2,1,0:T(8,128)(2,1)} %get-tuple-element.14.key, f32[2,7,8,128]{3,2,1,0:T(8,128)} %reshape.50.taps, f32[16,8,128]{2,1,0:T(8,128)} %bitcast.25, f32[8,128]{1,0:T(8,128)} %broadcast_in_dim.19.live), custom_call_target="tpu_custom_call" | custom-call | tf_op jit(solution)/shard_map/pallas_call | solution.py:432
  138.3 8.0 %shard_map.93.ends = f32[4,16,8,128]{3,2,1,0:T(8,128)} custom-call(f32[16,8,128]{2,1,0:T(8,128)} %get-tuple-element.16.mine), custom_call_target="tpu_custom_call" | custom-call | tf_op jit(solution)/shard_map/pallas_call | solution.py:437
  146.3 0.6 copy.11
  147.0 0.6 copy.12
  147.6 0.0 copy-done
  147.6 0.6 dynamic-slice_bitcast_fusion.skip
  148.2 0.7 broadcast_in_dim.20.earlier
  148.9 8.7 %shard_map.94.mine = bf16[512,1024]{1,0:T(8,128)(2,1)} custom-call(f32[4096,128]{1,0:T(8,128)} %get-tuple-element.15.spread, f32[4,16,8,128]{3,2,1,0:T(8,128)} %shard_map.93.ends, f32[3,8,128]{2,1,0:T(8,128)} %broadcast_in_dim.20.earlier, f32[16,8,128]{2,1,0:T(8,128)} %bitcast.27, f32[16,8,128]{2,1,0:T(8,128)} %bitcast.26, f32[16,8,128]{2,1,0:T(8,128)} %bitcast.28, ...), custom_call_target="tpu_custom_call" | custom-call | tf_op jit(solution)/shard_map/pallas_call | solution.py:438
  157.6 12.8 %shard_map.95 = bf16[128,4096]{1,0:T(8,128)(2,1)} custom-call(bf16[512,1024]{1,0:T(8,128)(2,1)} %shard_map.94.mine), custom_call_target="tpu_custom_call" | custom-call | tf_op jit(solution)/shard_map/pallas_call | solution.py:444
  170.4 0.0 copy-start.1
  170.4 0.0 copy-done.3
  170.5 0.0 copy-done.2
  170.5 0.3 maximum_convert_fusion
  170.8 1.5 fusion.8
  172.3 0.0 copy-done.1
  172.3 2.7 %fusion.2 = bf16[128,4096]{1,0:T(8,128)(2,1)} fusion(f32[134,4096]{1,0:T(8,128)S(1)} %maximum_convert_fusion, bf16[128,4096]{1,0:T(8,128)(2,1)S(1)} %copy-done.1, f32[4096]{0:T(1024)S(1)} %bitcast.35, f32[4096]{0:T(1024)S(1)} %bitcast.30, f32[4096]{0:T(1024)S(1)} %bitcast.31, f32[4096]{0:T(1024)S(1)} %bitcast.32, f32[4096]{0:T(1024)S(1)} %bitcast.33, ...), kind=kLoop, calls=%fused_computation.3 | loop fusion | flops 8388608 | bytes 16891904 | tf_op jit(solution)/shard_map/convert_element_type | solution.py:448
  (6 shorter events, 0.0 us)
Async XLA Ops:
  0.0 147.6 %copy-start = (f32[4096]{0:T(1024)S(1)}, f32[4096]{0:T(1024)}, u32[]{:S(2)}) copy-start(f32[4096]{0:T(1024)} %param.17) | copy-start | bytes 49156
  148.9 21.5 %copy-start.3 = (bf16[16,4096]{1,0:T(8,128)(2,1)S(1)}, bf16[16,4096]{1,0:T(8,128)(2,1)}, u32[]{:S(2)}) copy-start(bf16[16,4096]{1,0:T(8,128)(2,1)} %get-tuple-element.11) | copy-start | bytes 393220
  148.9 21.6 %copy-start.2 = (bf16[128,4096]{1,0:T(8,128)(2,1)S(1)}, bf16[128,4096]{1,0:T(8,128)(2,1)}, u32[]{:S(2)}) copy-start(bf16[128,4096]{1,0:T(8,128)(2,1)} %query.1) | copy-start | bytes 3145732
  170.4 1.9 %copy-start.1 = (bf16[128,4096]{1,0:T(8,128)(2,1)S(1)}, bf16[128,4096]{1,0:T(8,128)(2,1)}, u32[]{:S(2)}) copy-start(bf16[128,4096]{1,0:T(8,128)(2,1)} %shard_map.95) | copy-start | bytes 3145732

commit v4 on v3

--- a/solution.py
+++ b/solution.py
@@ -296,8 +296,24 @@
     )
 
 
-def end_states(value, key, taps, decay, live, spread, states, values, keys):
+def tile_of(source, row, target, place):
+    tall, lanes = target.shape[-2:]
+    start = where_am_i()[1] * (tall * lanes)
+    for column in range(tall):
+        cols = pl.ds(pl.multiple_of(start + column * lanes, lanes), lanes)
+        target[(*place, pl.ds(column, 1))] = source[(*row, cols)]
+
+
+def end_states(
+    value, key, all_taps, all_rates, spread, states, values, keys, taps, decay
+):
     modes, tall, lanes = decay.shape
+    for mode in range(modes):
+        tile_of(all_rates, (pl.ds(mode, 1),), decay, (mode,))
+        decay[mode] = jnp.exp(-decay[mode])
+    for branch in range(2):
+        for tap in range(taps.shape[1]):
+            tile_of(all_taps, (branch + 1, pl.ds(tap, 1)), taps, (branch, tap))
     margin = value.shape[0] - spread.shape[0] // tall
     count, rows = taps.shape[1], spread.shape[0] // tall
     piece = key.shape[1] - margin
@@ -322,7 +338,7 @@
             lay(keys, margin + part * piece + start,
                 lambda cols: key[part, pl.ds(margin + start, 16), cols])
 
-    on = live[...]
+    on = (where_am_i()[0] > 0).astype(jnp.float32)
     for row in range(margin):
         for target in (values, keys):
             place = slice(row * tall, (row + 1) * tall)
@@ -353,12 +369,17 @@
         states[mode] = held[mode]
 
 
-def run_states(spread, ends, earlier, block, decay, weight, skip, out, kept):
-    modes, tall, lanes = decay.shape
+def run_states(spread, ends, all_rates, residues, skip, out, kept, rate, weight, gains):
+    modes, tall, lanes = rate.shape
     rows = out.shape[0]
-    rates = [decay[mode] for mode in range(modes)]
-    weights = [weight[mode] for mode in range(modes)]
-    gain = skip[...]
+    plane = where_am_i()[0]
+    for mode in range(modes):
+        tile_of(all_rates, (pl.ds(mode, 1),), rate, (mode,))
+        tile_of(residues, (pl.ds(mode, 1),), weight, (mode,))
+    tile_of(skip, (pl.ds(0, 1),), gains, ())
+    rates = [jnp.exp(-rate[mode]) for mode in range(modes)]
+    weights = [weight[mode] * jnp.sqrt(rate[mode]) for mode in range(modes)]
+    gain = gains[...]
 
     def step(at, held):
         for part in range(4):
@@ -376,7 +397,8 @@
     for mode in range(modes):
         total = jnp.zeros((tall, lanes), jnp.float32)
         for at in range(ends.shape[0] - 1):
-            total = jnp.where(earlier[at] > 0, total * block[mode] + ends[at, mode], total)
+            longer = total * jnp.exp(-rate[mode] * rows) + ends[at, mode]
+            total = jnp.where(at < plane, longer, total)
         carried.append(total)
     lax.fori_loop(0, rows // 4, step, carried)
 
@@ -417,30 +439,25 @@
     value = jnp.dot(
         low_all, rows_all.reshape(both, width), preferred_element_type=jnp.float32).astype(half)
 
-    def mine(part):
-        return lax.dynamic_slice_in_dim(part, spot * width, width, part.ndim - 1)
-
     tiles, tile = (modes, tall, 128), (tall, 128)
-    rates, weights = mine(mode_rates), mine(residues)
-    weights = (weights * jnp.sqrt(rates)).reshape(tiles)
-    rates = rates.reshape(tiles)
-    decay, block = jnp.exp(-rates), jnp.exp(-rates * all_rows)
-    taps = mine(short_taps[1:]).reshape(2, margin_rows + 1, *tile)
-    order = jnp.arange(GROUP - 1)[:, None, None]
-    earlier = jnp.broadcast_to((order < plane).astype(jnp.float32), (GROUP - 1, *tile))
     scattered = pltpu.VMEM(((margin + all_rows) * tall, 128), jnp.float32)
     spread, states = pl.pallas_call(
         end_states,
         out_shape=[shape((all_rows * tall, 128), jnp.float32), shape(tiles, jnp.float32)],
-        in_specs=[VMEM] * 5, out_specs=[VMEM] * 2, scratch_shapes=[scattered, scattered],
-    )(value, key_all, taps, decay, earlier[0])
+        in_specs=[VMEM] * 4, out_specs=[VMEM] * 2,
+        scratch_shapes=[
+            scattered, scattered, pltpu.VMEM((2, margin_rows + 1, *tile), jnp.float32),
+            pltpu.VMEM(tiles, jnp.float32)],
+    )(value, key_all, short_taps, mode_rates)
     ends = talk(share_states, shape((GROUP, *tiles), jnp.float32), [VMEM], [], 3, 1, 2)(states)
     mixed_out = pl.pallas_call(
         run_states,
         out_shape=shape((all_rows, width), half),
-        in_specs=[VMEM] * 7, out_specs=VMEM,
-        scratch_shapes=[pltpu.VMEM((all_rows * tall, 128), jnp.float32)],
-    )(spread, ends, earlier, block, decay, weights, mine(skip_gain).reshape(tile))
+        in_specs=[VMEM] * 5, out_specs=VMEM,
+        scratch_shapes=[
+            pltpu.VMEM((all_rows * tall, 128), jnp.float32), pltpu.VMEM(tiles, jnp.float32),
+            pltpu.VMEM(tiles, jnp.float32), pltpu.VMEM(tile, jnp.float32)],
+    )(spread, ends, mode_rates, residues, skip_gain[None])
     given = talk(give_back, shape((rows, channels), half), [VMEM], [], 3, 1, 3)(mixed_out)
     first = lax.axis_index("seq") == 0
     query_previous = jnp.where(first, 0, query_edge[margin - margin_rows:]).astype(half)

time: 175 us -> 170 us (0.971)
  local copies, waits for them, and re-layouts: 6.92 us -> 1.53 us
    unnamed x11 -> x6, local copies, waits for them, and re-layouts: 1.93 us -> 0.01 us
where the time goes in v4:
time: 170 us
  Pallas kernels  160 us (94%)
  matrix products  5.22 us (3%)
  other arithmetic  3.02 us (2%)
    pallas_call x1, Pallas kernels, planes_device(): talk(fetch_all, [shape((margin + all_rows, both), half), shape((GROUP, GR...  120 us
    pallas_call x1, Pallas kernels, planes_device(): talk(give_back, shape((rows, channels), half), [VMEM], [], 3, 1, 3)  12.9 us
    pallas_call x1, Pallas kernels, planes_device(): pl.pallas_call(end_states, out_shape=[shape((all_rows * tall, 128), jnp.f...  9.66 us
    pallas_call x1, Pallas kernels, planes_device(): pl.pallas_call(run_states, out_shape=shape((all_rows, width), half), in_s...  8.93 us
    pallas_call x1, Pallas kernels, planes_device(): talk(share_states, shape((GROUP, *tiles), jnp.float32), [VMEM], [], 3, 1, 2)  8 us
    dot_general x1, matrix products, planes_device(): jnp.dot(low_all, rows_all.reshape(both, width), preferred_element_type=jn...  5.22 us

profile of v4, /device:TPU:0, one launch (start us, length us, event | category | flops | bytes accessed | tf_op | source)
XLA Modules:
  0.0 169.6 jit_solution(6662131241462523641)
XLA Ops:
  0.0 120.2 %shard_map.91 = (bf16[528,1536]{1,0:T(8,128)(2,1)}, bf16[4,4,96,1024]{3,2,1,0:T(8,128)(2,1)}, bf16[4,144,1024]{2,1,0:T(8,128)(2,1)}, bf16[16,4096]{1,0:T(8,128)(2,1)}) custom-call(bf16[128,4096]{1,0:T(8,128)(2,1)} %tok.1, bf16[96,4096]{1,0:T(8,128)(2,1)} %bitcast.12, bf16[96,4096]{1,0:T(8,128)(2,1)} %pout.1, bf16[128,4096]{1,0:T(8,128)(2,1)} %key.1, ...), custom_call_target="tpu_custom_call" | custom-call | tf_op jit(solution)/shard_map/pallas_call | solution.py:428
  120.2 5.2 %convolution_convert_fusion.value = bf16[528,1024]{1,0:T(8,128)(2,1)} fusion(bf16[528,1536]{1,0:T(8,128)(2,1)} %get-tuple-element.12, bf16[1536,1024]{1,0:T(8,128)(2,1)} %bitcast.21), kind=kOutput, calls=%fused_computation.15 | convolution fusion | flops 1661485056 | bytes 5849088 | tf_op jit(solution)/shard_map/dot_general | solution.py:439
  125.5 9.7 %shard_map.92 = (f32[4096,128]{1,0:T(8,128)}, f32[16,8,128]{2,1,0:T(8,128)}) custom-call(bf16[528,1024]{1,0:T(8,128)(2,1)} %convolution_convert_fusion.value, bf16[4,144,1024]{2,1,0:T(8,128)(2,1)} %get-tuple-element.14.key, f32[3,7,4096]{2,1,0:T(8,128)} %all_taps.1, f32[16,4096]{1,0:T(8,128)} %all_rates.3), custom_call_target="tpu_custom_call" | custom-call | tf_op jit(solution)/shard_map/pallas_call | solution.py:444
  135.1 8.0 %shard_map.93.ends = f32[4,16,8,128]{3,2,1,0:T(8,128)} custom-call(f32[16,8,128]{2,1,0:T(8,128)} %get-tuple-element.16.mine), custom_call_target="tpu_custom_call" | custom-call | tf_op jit(solution)/shard_map/pallas_call | solution.py:452
  143.1 8.9 %shard_map.94.mine = bf16[512,1024]{1,0:T(8,128)(2,1)} custom-call(f32[4096,128]{1,0:T(8,128)} %get-tuple-element.15.spread, f32[4,16,8,128]{3,2,1,0:T(8,128)} %shard_map.93.ends, f32[16,4096]{1,0:T(8,128)} %all_rates.3, f32[16,4096]{1,0:T(8,128)} %residues.1, f32[1,4096]{1,0:T(1,128)} %bitcast.20), custom_call_target="tpu_custom_call" | custom-call | tf_op jit(solution)/shard_map/pallas_call | solution.py:453
  152.1 0.0 copy-start.2
  152.1 0.0 copy-start.1
  152.1 12.9 %shard_map.95 = bf16[128,4096]{1,0:T(8,128)(2,1)} custom-call(bf16[512,1024]{1,0:T(8,128)(2,1)} %shard_map.94.mine), custom_call_target="tpu_custom_call" | custom-call | tf_op jit(solution)/shard_map/pallas_call | solution.py:461
  165.0 0.0 copy-start
  165.0 1.5 fusion.8
  166.5 0.0 copy-done.2
  166.5 0.0 copy-done.1
  166.5 0.3 maximum_convert_fusion
  166.8 0.0 copy-done
  166.8 2.7 %fusion.2 = bf16[128,4096]{1,0:T(8,128)(2,1)} fusion(f32[134,4096]{1,0:T(8,128)S(1)} %maximum_convert_fusion, bf16[128,4096]{1,0:T(8,128)(2,1)S(1)} %copy-done, f32[4096]{0:T(1024)S(1)} %bitcast.19, f32[4096]{0:T(1024)S(1)} %bitcast.14, f32[4096]{0:T(1024)S(1)} %bitcast.15, f32[4096]{0:T(1024)S(1)} %bitcast.16, f32[4096]{0:T(1024)S(1)} %bitcast.17, ...), kind=kLoop, calls=%fused_computation.3 | loop fusion | flops 8388608 | bytes 16891904 | tf_op jit(solution)/shard_map/convert_element_type | solution.py:465
  (1 shorter events, 0.0 us)
Async XLA Ops:
  152.1 14.4 %copy-start.2 = (bf16[16,4096]{1,0:T(8,128)(2,1)S(1)}, bf16[16,4096]{1,0:T(8,128)(2,1)}, u32[]{:S(2)}) copy-start(bf16[16,4096]{1,0:T(8,128)(2,1)} %get-tuple-element.11) | copy-start | bytes 393220
  152.1 14.5 %copy-start.1 = (bf16[128,4096]{1,0:T(8,128)(2,1)S(1)}, bf16[128,4096]{1,0:T(8,128)(2,1)}, u32[]{:S(2)}) copy-start(bf16[128,4096]{1,0:T(8,128)(2,1)} %query.1) | copy-start | bytes 3145732
  165.0 1.9 %copy-start = (bf16[128,4096]{1,0:T(8,128)(2,1)S(1)}, bf16[128,4096]{1,0:T(8,128)(2,1)}, u32[]{:S(2)}) copy-start(bf16[128,4096]{1,0:T(8,128)(2,1)} %shard_map.95) | copy-start | bytes 3145732
